TPU v7x, 32 devices: a whole 2x2x4 slice. The times are simulated.
32 devices in a mesh: groups: 2 (over y), dp: 4 (over z), section: 2 (over x), tensor: 2 (over core).
Axes of the slice: x: 2, y: 2, z: 4, core: 2. Of those that a mesh axis runs over, the one named last changes fastest.
Arguments:
- hidden: bfloat16 [128, 8, 5120], P(('groups', 'dp')), parts along dimension 0, may hold values from -6 to 6
- unembed: bfloat16 [128, 8, 5120], P(('groups', 'dp')), parts along dimension 0, may hold values from -0.02734375 to 0.02734375
- value_proj: bfloat16 [2, 5120, 512], P('section', 'dp', 'tensor'), may hold values from -0.078125 to 0.078125
- output_proj: bfloat16 [2, 512, 5120], P('section', 'tensor', 'dp'), may hold values from -0.125 to 0.125
- norm_gains: float32 [2, 5120], P('section'), may hold values from 0.1 to 1.9
- survive: int32 [8], P(('groups', 'dp')), parts along dimension 0, may hold values from 0 to 1, as said below
- lengths: int32 [128], P(('groups', 'dp')), parts along dimension 0, may hold values from 1 to 8
- assign: int32 [128], P(('groups', 'dp')), parts along dimension 0, may hold values from 0 to 16, as said below
- advantage: float32 [128], P(('groups', 'dp')), parts along dimension 0, may hold values from -4 to 4
- reference_logit: float32 [128, 8], P(('groups', 'dp')), parts along dimension 0, may hold values from -4 to 4
- recorded_gap: float32 [128, 8], P(('groups', 'dp')), parts along dimension 0, may hold values from -2 to 2
Outputs:
- grad_value: float32 [4, 5120, 512], P(('groups', 'section'), 'dp', 'tensor'), parts along dimension 0
- grad_output: float32 [4, 512, 5120], P(('groups', 'section'), 'tensor', 'dp'), parts along dimension 0
There are 2 independent parts, one for each index of `groups`. A program takes and returns all parts, laid end to end along the dimension named above; an argument that names none is the same for every part. Nothing has to cross between parts.
Inputs may be any that keep to these rules, and one draw needn't show every extreme that they name: `survive`: 1 where the group of 16 responses is kept, 0 where it is dropped; in every draw all groups of some dp index are kept. `assign`: the 16 slots of a dp index list the local positions (0 to 15) of the responses of its kept groups, each exactly once, then hold 16 in every other slot.
All inputs are finite; a program needn't handle non-finite values.
Results may differ from a plain program's by a relative error of at most 0.029.
Values may be sent and summed in bfloat16 or wider, within the bound.
A program may use at most 64 MiB of HBM per device.

v0:
```python
import functools
import math

import jax
import jax.numpy as jnp
from jax import lax
from jax.experimental import pallas as pl
from jax.experimental.pallas import tpu as pltpu
from jax.sharding import PartitionSpec as P

eps_norm = 1e-06
loss_scale = 4096.0
clip_high = math.log(1.28)
clip_low = math.log(0.8)
LANES = 128
KINDS = ("a", "xf", "uf", "p", "q", "pj", "pjf", "gq", "gqf", "sc", "tk", "x", "g", "w", "e", "ps")
BF = jnp.bfloat16
F32 = jnp.float32


def dot(a, b, ca=1, cb=0):
    return lax.dot_general(a, b, (((ca,), (cb,)), ((), ())), preferred_element_type=F32)


def kernel(
    n, sections, width,
    src, w1, w2, gains, survive, lengths, assign, advantage, base, gap,
    dw1, dw2,
    xs, us, xg, pb, pr, qb, qr, pj, gq, sc, w1o, w2o, yx, yg, tk, exs, exr, pacc, qacc, rkeep,
    ps, psr, rinfo, tok,
    ss, rs,
):
    j = lax.axis_index("dp")
    s = lax.axis_index("section")
    t = lax.axis_index("tensor")
    o = 1 - t
    rows = src.shape[1]
    half, v = w1.shape[1:]
    last = sections - 1
    partner = {"tensor": o}
    positions, count = base.shape

    def gain(h):
        return gains[j * 2 + h]

    def own_tokens():
        response = lax.broadcasted_iota(jnp.int32, (1, count), 1)
        group = count // survive.shape[1]
        kept = jnp.zeros((1, count), F32)
        for g in range(survive.shape[1]):
            inside = (response >= g * group) & (response < (g + 1) * group)
            kept = jnp.where(inside, survive[0:1, g:g + 1].astype(F32), kept)
        held = jnp.sum(kept * lengths[...].astype(F32), axis=1, keepdims=True)
        tok[...] = jnp.broadcast_to(held, (8, LANES))

    def row_info():
        row = lax.broadcasted_iota(jnp.int32, (rows, count), 0)
        first = lax.broadcasted_iota(jnp.int32, (rows, count), 1) * positions
        mine = (row >= first) & (row < first + positions)

        def by_response(values):
            return jnp.sum(jnp.where(mine, values, 0.0), axis=1, keepdims=True)

        def by_position(values):
            return by_response(jnp.concatenate([values] * count, axis=0))

        slots = assign[...]
        starts = slots * positions
        hit = (row >= starts) & (row < starts + positions)
        listed = jnp.sum(jnp.where(hit, 1.0, 0.0), axis=1, keepdims=True)
        start = by_response(first.astype(F32))
        place = lax.broadcasted_iota(jnp.int32, (rows, 1), 0).astype(F32) - start
        live = place < by_response(lengths[...].astype(F32))
        adv = by_response(advantage[...])
        q = by_position(gap[...])
        clipped = ((adv > 0) & (q > clip_high)) | ((adv < 0) & (q < clip_low))
        weight = jnp.where(clipped | (~live), 0.0, -loss_scale * adv * listed)
        rinfo[...] = jnp.where(lane == 0, weight, jnp.where(lane == 1, by_position(base[...]), 0.0))

    def blk(b):
        return pl.ds(pl.multiple_of(b * rows, rows), rows)

    def peer(k):
        return lax.rem(j + k, n)

    def send(kind, si, ri, a, b, dev):
        k = KINDS.index(kind)
        pltpu.make_async_remote_copy(
            src_ref=a, dst_ref=b, send_sem=ss.at[k, si], recv_sem=rs.at[k, ri],
            device_id=dev, device_id_type=pl.DeviceIdType.MESH,
        ).start()

    def handle(kind, i, a):
        k = KINDS.index(kind)
        return pltpu.make_async_remote_copy(
            src_ref=a, dst_ref=a, send_sem=ss.at[k, i], recv_sem=rs.at[k, i],
            device_id=partner, device_id_type=pl.DeviceIdType.MESH,
        )

    def got(kind, i, a):
        handle(kind, i, a).wait_recv()

    def sent(kind, i, a):
        handle(kind, i, a).wait_send()

    def others(body):
        def step(k, carry):
            body(peer(k))
            return carry
        lax.fori_loop(1, n, step, 0)

    def everyone(body):
        def step(k, carry):
            body(peer(k))
            return carry
        lax.fori_loop(0, n, step, 0)

    barrier = pltpu.get_barrier_semaphore()

    def greet(dev):
        pl.semaphore_signal(barrier, inc=1, device_id=dev, device_id_type=pl.DeviceIdType.MESH)

    for k in range(1, n):
        greet({"dp": peer(k)})
    greet(partner)

    @pl.when(s > 0)
    def _():
        greet({"section": s - 1})

    @pl.when(s < last)
    def _():
        greet({"section": s + 1})

    pl.semaphore_wait(barrier, n + jnp.where(s > 0, 1, 0) + jnp.where(s < last, 1, 0))

    def start_common():
        send("w", 0, 0, w1.at[o], w1o, partner)
        send("w", 1, 1, w2.at[o], w2o, partner)
        own_tokens()
        others(lambda b: send("tk", b, j, tok, tk.at[j], {"dp": b}))
        tk[j] = tok[...]

    def all_to_all(dst):
        others(lambda b: send("a", b, j, src.at[b * 2 + t], dst.at[t, blk(j)], {"dp": b}))
        dst[0, blk(j)] = src[j * 2]
        dst[1, blk(j)] = src[j * 2 + 1]

    def arrive(kind, fkind, buf, b):
        got(kind, b, buf.at[t, blk(b)])
        send(fkind, b, b, buf.at[t, blk(b)], buf.at[t, blk(b)], partner)
        got(fkind, b, buf.at[o, blk(b)])

    lane = lax.broadcasted_iota(jnp.int32, (rows, LANES), 1)

    def pack(values):
        packed = jnp.zeros((rows, LANES), F32)
        for i, value in enumerate(values):
            packed = jnp.where(lane == i, value, packed)
        return packed.T[:8]

    def unpack(packed):
        filled = jnp.concatenate([packed, jnp.zeros((LANES - 8, rows), F32)], axis=0)
        return filled.T

    def forward_chunk(b, with_logit):
        total = jnp.zeros((rows, v), F32)
        squares = jnp.zeros((rows, 1), F32)
        logit = jnp.zeros((rows, 1), F32)
        for h in range(2):
            x = xs[h, blk(b)].astype(F32)
            squares += jnp.sum(x * x, axis=1, keepdims=True)
            if with_logit:
                logit += jnp.sum(x * us[h, blk(b)].astype(F32), axis=1, keepdims=True)
            scaled = (x * gain(h)).astype(BF)
            xg[h, blk(b)] = scaled
            total += dot(scaled, w1[h])
        pb[blk(b)] = total.astype(BF)
        ps[b] = pack([squares, logit] if with_logit else [squares])

        @pl.when(b != j)
        def _():
            send("p", b, j, pb.at[blk(b)], pr.at[j], {"dp": b})
            send("ps", b, j, ps.at[b], psr.at[j], {"dp": b})

    def backward_chunk(b):
        total = dot(us[0, blk(b)], w2[0], 1, 1) + dot(us[1, blk(b)], w2[1], 1, 1)
        qb[blk(b)] = total.astype(BF)

        @pl.when(b != j)
        def _():
            send("q", b, j, qb.at[blk(b)], qr.at[j], {"dp": b})

    def reduce(kind, own, landed, acc):
        acc[...] = own[blk(j)].astype(F32)

        def add(b):
            got(kind, b, landed.at[b])
            acc[...] += landed[b].astype(F32)
        others(add)

    def share(kind, buf, forward):
        others(lambda b: send(kind, b, j, buf.at[t, blk(j)], buf.at[t, blk(j)], {"dp": b}))
        if forward:
            send(kind + "f", j, j, buf.at[t, blk(j)], buf.at[t, blk(j)], partner)

    def shared(kind, buf, b):
        @pl.when(b != j)
        def _():
            got(kind, b, buf.at[t, blk(b)])
            send(kind + "f", b, b, buf.at[t, blk(b)], buf.at[t, blk(b)], partner)
        got(kind + "f", b, buf.at[o, blk(b)])

    def own_inverse():
        psr[j] = ps[j]
        others(lambda b: got("ps", b, psr.at[b]))
        sums = psr[0]
        for b in range(1, n):
            sums = sums + psr[b]
        sums = unpack(sums)
        inverse = lax.rsqrt(sums[:, 0:1] / width + eps_norm)
        rkeep[...] = jnp.where(lane == 0, inverse, sums)
        return inverse

    def forward_out():
        inverse = own_inverse()
        reduce("p", pb, pr, pacc)
        pj[t, blk(j)] = (inverse * pacc[...]).astype(BF)
        share("pj", pj, True)
        got("w", 1, w2o)

        def chunk(b):
            shared("pj", pj, b)
            mixed = dot(pj[t, blk(b)], w2[t]) + dot(pj[o, blk(b)], w2o[...])
            yx[blk(b)] = (xs[t, blk(b)].astype(F32) + mixed).astype(BF)
            send("x", b, b, yx.at[blk(b)], xs.at[t, blk(b)], {"section": s + 1})
        everyone(chunk)

    def dot_over_units():
        exs[...] = jnp.broadcast_to(
            jnp.sum(pacc[...] * qacc[...], axis=1, keepdims=True), (rows, LANES)
        )
        send("e", 0, 0, exs, exr, partner)
        got("e", 0, exr)
        return exs[:, :1] + exr[:, :1]

    def backward_out(is_last):
        reduce("q", qb, qr, qacc)
        inner = dot_over_units()
        inverse = rkeep[:, :1]
        if is_last:
            logit = rkeep[:, 1:2] + inverse * inner
            seed = rinfo[:, 0:1] * jnp.exp(logit - rinfo[:, 1:2])
            scale = seed * inverse
            pj[t, blk(j)] = (scale * pacc[...]).astype(BF)
        else:
            seed = jnp.ones((rows, 1), F32)
            scale = inverse
        gq[t, blk(j)] = (scale * qacc[...]).astype(BF)
        sc[j] = pack([inverse * inverse * inverse * (seed * inner) / width, seed])
        share("gq", gq, True)
        others(lambda b: send("sc", b, j, sc.at[j], sc.at[j], {"dp": b}))
        got("w", 0, w1o)

        def chunk(b):
            shared("gq", gq, b)

            @pl.when(b != j)
            def _():
                got("sc", b, sc.at[b])
            packed = unpack(sc[b])
            grad = dot(gq[t, blk(b)], w1[t], 1, 1) + dot(gq[o, blk(b)], w1o[...], 1, 1)
            upstream = us[t, blk(b)].astype(F32)
            if is_last:
                upstream = packed[:, 1:2] * upstream
            yg[blk(b)] = (
                upstream + gain(t) * grad - packed[:, 0:1] * xs[t, blk(b)].astype(F32)
            ).astype(BF)
            send("g", b, b, yg.at[blk(b)], us.at[t, blk(b)], {"section": s - 1})
        everyone(chunk)

    def tokens():
        others(lambda b: got("tk", b, tk.at[b]))
        count = tk[0]
        for b in range(1, n):
            count = count + tk[b]
        return 1.0 / count[0:1, 0:1]

    def finish_value(scale):
        for h in range(2):
            dw1[h] = dot(xg[h], gq[t], 0, 0) * scale

    def finish_value_arriving(scale):
        def add(b, start):
            for h in range(2):
                part = dot(xg[h, blk(b)], gq[t, blk(b)], 0, 0) * scale
                dw1[h] = part if start else dw1[h] + part
        add(j, True)

        def later(b):
            got("gq", b, gq.at[t, blk(b)])
            add(b, False)
        others(later)

    def finish_output(scale):
        for h in range(2):
            dw2[:, h * half:(h + 1) * half] = dot(pj[t], us[h], 0, 0) * scale

    def drain_common():
        sent("w", 0, w1o)
        sent("w", 1, w2o)

        def one(b):
            sent("tk", b, tk.at[b])
            sent("p", b, pb.at[blk(b)])
            sent("ps", b, ps.at[b])
            sent("q", b, qb.at[blk(b)])
            sent("pj", b, pj.at[t, blk(b)])
            sent("gq", b, gq.at[t, blk(b)])
        others(one)

    def first_section():
        start_common()
        all_to_all(xs)
        forward_chunk(j, False)

        def chunk(b):
            arrive("a", "xf", xs, b)
            forward_chunk(b, False)
        others(chunk)
        forward_out()

        def back(b):
            arrive("g", "uf", us, b)
            backward_chunk(b)
        everyone(back)
        scale = tokens()
        reduce("q", qb, qr, qacc)
        gq[t, blk(j)] = (rkeep[:, :1] * qacc[...]).astype(BF)
        share("gq", gq, False)
        finish_output(scale)
        finish_value_arriving(scale)
        got("w", 0, w1o)
        drain_common()

        def rest(b):
            sent("a", b, src.at[0])
            sent("xf", b, xs.at[t, blk(b)])
        others(rest)

        def rest_all(b):
            sent("pjf", b, pj.at[t, blk(b)])
            sent("x", b, yx.at[blk(b)])
            sent("uf", b, us.at[t, blk(b)])
        everyone(rest_all)

    def middle_section():
        start_common()

        def chunk(b):
            arrive("x", "xf", xs, b)
            forward_chunk(b, False)
        everyone(chunk)
        forward_out()

        def back(b):
            arrive("g", "uf", us, b)
            backward_chunk(b)
        everyone(back)
        backward_out(False)
        scale = tokens()
        finish_output(scale)
        finish_value(scale)
        drain_common()
        sent("e", 0, exs)
        others(lambda b: sent("sc", b, sc.at[b]))

        def rest_all(b):
            sent("xf", b, xs.at[t, blk(b)])
            sent("uf", b, us.at[t, blk(b)])
            sent("pjf", b, pj.at[t, blk(b)])
            sent("gqf", b, gq.at[t, blk(b)])
            sent("x", b, yx.at[blk(b)])
            sent("g", b, yg.at[blk(b)])
        everyone(rest_all)

    def last_section():
        start_common()
        all_to_all(us)
        backward_chunk(j)
        row_info()

        def seeds(b):
            arrive("a", "uf", us, b)
            backward_chunk(b)
        others(seeds)

        def chunk(b):
            arrive("x", "xf", xs, b)
            forward_chunk(b, True)
        everyone(chunk)
        own_inverse()
        reduce("p", pb, pr, pacc)
        backward_out(True)
        share("pj", pj, False)
        scale = tokens()
        finish_value(scale)
        others(lambda b: got("pj", b, pj.at[t, blk(b)]))
        finish_output(scale)
        got("w", 1, w2o)
        drain_common()
        sent("e", 0, exs)

        def rest(b):
            sent("a", b, src.at[0])
            sent("uf", b, us.at[t, blk(b)])
            sent("sc", b, sc.at[b])
        others(rest)

        def rest_all(b):
            sent("xf", b, xs.at[t, blk(b)])
            sent("gqf", b, gq.at[t, blk(b)])
            sent("g", b, yg.at[blk(b)])
        everyone(rest_all)

    pl.when(s == 0)(first_section)
    pl.when(s == last)(last_section)
    if sections > 2:
        pl.when((s > 0) & (s < last))(middle_section)


def local(
    hidden, unembed, value_proj, output_proj, norm_gains, survive, lengths, assign,
    advantage, reference_logit, recorded_gap,
):
    n = lax.axis_size("dp")
    sections = lax.axis_size("section")
    s = lax.axis_index("section")
    count, positions, width = hidden.shape
    rows = count * positions
    part = value_proj.shape[1]
    half = part // 2
    v = value_proj.shape[2]

    src = jnp.where(s == sections - 1, unembed, hidden).reshape(rows, n * 2, half)
    src = src.transpose(1, 0, 2)
    w1 = value_proj[0].reshape(2, half, v)
    w2 = output_proj[0].reshape(v, 2, half).transpose(1, 0, 2)
    gains = norm_gains[0].reshape(n * 2, 1, half)
    total = n * rows
    kinds = len(KINDS)
    vm = pl.BlockSpec(memory_space=pltpu.VMEM)
    dw1, dw2 = pl.pallas_call(
        functools.partial(kernel, n, sections, width),
        out_shape=(
            jax.ShapeDtypeStruct((2, half, v), F32),
            jax.ShapeDtypeStruct((v, part), F32),
        ),
        in_specs=[vm] * 10,
        out_specs=(vm, vm),
        scratch_shapes=[
            pltpu.VMEM((2, total, half), BF),
            pltpu.VMEM((2, total, half), BF),
            pltpu.VMEM((2, total, half), BF),
            pltpu.VMEM((total, v), BF),
            pltpu.VMEM((n, rows, v), BF),
            pltpu.VMEM((total, v), BF),
            pltpu.VMEM((n, rows, v), BF),
            pltpu.VMEM((2, total, v), BF),
            pltpu.VMEM((2, total, v), BF),
            pltpu.VMEM((n, 8, rows), F32),
            pltpu.VMEM((half, v), BF),
            pltpu.VMEM((v, half), BF),
            pltpu.VMEM((total, half), BF),
            pltpu.VMEM((total, half), BF),
            pltpu.VMEM((n, 8, LANES), F32),
            pltpu.VMEM((rows, LANES), F32),
            pltpu.VMEM((rows, LANES), F32),
            pltpu.VMEM((rows, v), F32),
            pltpu.VMEM((rows, v), F32),
            pltpu.VMEM((rows, LANES), F32),
            pltpu.VMEM((n, 8, rows), F32),
            pltpu.VMEM((n, 8, rows), F32),
            pltpu.VMEM((rows, LANES), F32),
            pltpu.VMEM((8, LANES), F32),
            pltpu.SemaphoreType.DMA((kinds, n)),
            pltpu.SemaphoreType.DMA((kinds, n)),
        ],
        compiler_params=pltpu.CompilerParams(
            collective_id=0, has_side_effects=True, vmem_limit_bytes=60 * 1024 * 1024
        ),
    )(
        src, w1, w2, gains, survive.reshape(1, -1), lengths.reshape(1, count),
        assign.reshape(1, count), advantage.reshape(1, count), reference_logit.T, recorded_gap.T,
    )
    return (
        dw1.reshape(1, part, v),
        dw2[None],
    )


def solution(mesh):
    rowwise = P(("groups", "dp"))
    placed = (
        P(("groups", "dp"), None, None),
        P(("groups", "dp"), None, None),
        P("section", "dp", "tensor"),
        P("section", "tensor", "dp"),
        P("section", None),
        rowwise,
        rowwise,
        rowwise,
        rowwise,
        P(("groups", "dp"), None),
        P(("groups", "dp"), None),
    )
    return jax.shard_map(
        local,
        mesh=mesh,
        in_specs=placed,
        out_specs=(
            P(("groups", "section"), "dp", "tensor"),
            P(("groups", "section"), "tensor", "dp"),
        ),
        check_vma=False,
    )
```

profile of v0, /device:TPU:0, one launch (start us, length us, event | category | flops | bytes accessed | tf_op | source)
XLA Modules:
  0.0 100.2 jit_solution(4252063793616444441)
XLA Ops:
  1.3 0.0 copy-start
  1.3 0.0 copy-start.1
  1.3 1.5 %copy.14 = bf16[1,256,1280]{1,2,0:T(8,128)(2,1)S(1)} copy(bf16[1,256,1280]{2,1,0:T(8,128)(2,1)} %param.14) | data formatting | bytes 1310720 | tf_op args[3]
  2.8 1.1 %copy.15 = bf16[256,2,640]{2,0,1:T(8,128)(2,1)} copy(bf16[256,2,640]{0,2,1:T(8,128)(2,1)S(1)} %bitcast.22) | data formatting | bytes 1310720 | tf_op jit(solution)/shard_map/reshape;squeeze | solution.py:448
  3.9 0.0 copy-done
  3.9 0.0 copy-done.1
  3.9 0.1 broadcast_select_fusion
  4.0 0.2 copy.16
  4.2 1.2 %copy.18 = bf16[128,8,640]{2,0,1:T(8,128)(2,1)} copy(bf16[128,8,640]{2,1,0:T(8,128)(2,1)S(1)} %bitcast.21) | data formatting | bytes 2621440 | tf_op jit(solution)/shard_map/reshape | solution.py:445
  5.4 91.1 %shard_map.122 = (f32[2,640,256]{2,1,0:T(8,128)}, f32[256,1280]{1,0:T(8,128)}) custom-call(bf16[8,128,640]{2,1,0:T(8,128)(2,1)} %bitcast.19, bf16[2,640,256]{2,1,0:T(8,128)(2,1)} %bitcast.26, bf16[2,256,640]{2,1,0:T(8,128)(2,1)} %bitcast.23, f32[8,1,640]{2,1,0:T(1,128)} %bitcast.27, s32[1,1]{1,0:T(1,128)} %bitcast.18.survive, s32[1,16]{1,0:T(1,128)} %bitcast.30, ...), custom_call_target="tpu_custom_call" | custom-call | tf_op jit(solution)/shard_map/pallas_call | solution.py:453
  96.5 0.0 copy-start.2
  96.6 2.6 %copy.22 = f32[1,1280,256]{2,1,0:T(8,128)} copy(f32[1,1280,256]{2,1,0:T(8,128)} %bitcast.25) | data formatting | bytes 2621440
  99.1 0.0 copy-done.2
  99.1 1.1 %copy.23 = f32[1,256,1280]{2,1,0:T(8,128)} copy(f32[1,256,1280]{2,1,0:T(8,128)S(1)} %bitcast.24) | data formatting | bytes 2621440
Async XLA Ops:
  1.3 2.6 %copy-start = (bf16[16,8,5120]{2,1,0:T(8,128)(2,1)S(1)}, bf16[16,8,5120]{2,1,0:T(8,128)(2,1)}, u32[]{:S(2)}) copy-start(bf16[16,8,5120]{2,1,0:T(8,128)(2,1)} %param.12) | copy-start | bytes 3932164
  1.3 2.6 %copy-start.1 = (bf16[16,8,5120]{2,1,0:T(8,128)(2,1)S(1)}, bf16[16,8,5120]{2,1,0:T(8,128)(2,1)}, u32[]{:S(2)}) copy-start(bf16[16,8,5120]{2,1,0:T(8,128)(2,1)} %param.11) | copy-start | bytes 3932164
  96.5 2.6 %copy-start.2 = (f32[256,1280]{1,0:T(8,128)S(1)}, f32[256,1280]{1,0:T(8,128)}, u32[]{:S(2)}) copy-start(f32[256,1280]{1,0:T(8,128)} %get-tuple-element.5) | copy-start | bytes 3932164
where the time goes:
time: 100 us
  Pallas kernels  91.1 us (91%)
  local copies, waits for them, and re-layouts  7.6 us (8%)
  between operations  1.33 us (1%)
    pallas_call x1, Pallas kernels, local(): pl.pallas_call(functools.partial(kernel, n, sections, width), out_shape=(...  91.1 us
    unnamed x10, local copies, waits for them, and re-layouts  5.31 us

commit v1 on v0

--- a/solution.py
+++ b/solution.py
@@ -429,7 +429,7 @@
         pl.when((s > 0) & (s < last))(middle_section)
 
 
-def local(
+def local_chain(
     hidden, unembed, value_proj, output_proj, norm_gains, survive, lengths, assign,
     advantage, reference_logit, recorded_gap,
 ):
@@ -499,6 +499,624 @@
     )
 
 
+PAIR_KINDS = (
+    "a", "af", "ax", "axf", "bx", "bf", "ax1", "af1", "gn", "mr", "mk", "rr", "rl", "ps", "p0", "s0",
+    "in", "w", "d1", "s1", "g0", "g0f", "g1", "g1f", "g2", "gs", "tk",
+)
+
+
+def pair_kernel(
+    n, width,
+    hid, une, w1, w2, gains, survive, lengths, assign, advantage, base, gap,
+    dw1, dw2,
+    xs, us, xg, wv1, wv2, b0f, a1f, b0g, gx, mp, mr, mk, part, own, rin, p0, dp1, gz, ga, gb,
+    wr, wsend, ps, psr, scs, scr, inn, inr, sc, rinfo, tok, tk,
+    ss, rs, ls,
+):
+    j = lax.axis_index("dp")
+    s = lax.axis_index("section")
+    t = lax.axis_index("tensor")
+    y = lax.axis_index("groups")
+    o = 1 - t
+    rows = hid.shape[0]
+    chunk, v = w1.shape
+    half = chunk // 2
+    mb = v // n
+    positions, count = base.shape
+    partner = {"tensor": o}
+    right = {"dp": j + 1}
+    left = {"dp": j - 1}
+    lane = lax.broadcasted_iota(jnp.int32, (rows, LANES), 1)
+
+    def blk(b):
+        return pl.ds(pl.multiple_of(b * rows, rows), rows)
+
+    def cols(h):
+        return pl.ds(pl.multiple_of(h * half, half), half)
+
+    def wide(b, h):
+        return pl.ds(pl.multiple_of(b * chunk + h * half, half), half)
+
+    def mrows(g, b):
+        return pl.ds(pl.multiple_of(g * v + b * mb, mb), mb)
+
+    def send(kind, si, ri, a, b, dev):
+        k = PAIR_KINDS.index(kind)
+        pltpu.make_async_remote_copy(
+            src_ref=a, dst_ref=b, send_sem=ss.at[k, si], recv_sem=rs.at[k, ri],
+            device_id=dev, device_id_type=pl.DeviceIdType.MESH,
+        ).start()
+
+    def handle(kind, i, a):
+        k = PAIR_KINDS.index(kind)
+        return pltpu.make_async_remote_copy(
+            src_ref=a, dst_ref=a, send_sem=ss.at[k, i], recv_sem=rs.at[k, i],
+            device_id=partner, device_id_type=pl.DeviceIdType.MESH,
+        )
+
+    def got(kind, i, a):
+        handle(kind, i, a).wait_recv()
+
+    def sent(kind, i, a):
+        handle(kind, i, a).wait_send()
+
+    def others(body):
+        def step(k, carry):
+            body(lax.rem(j + k, n))
+            return carry
+        lax.fori_loop(1, n, step, 0)
+
+    def at_distance(d, body):
+        pl.when(j + d < n)(lambda: body(j + d))
+        pl.when(j - d >= 0)(lambda: body(j - d))
+
+    def replicas(body):
+        def step(k, carry):
+            at = lax.rem(y * n + j + k, 2 * n)
+            body(at // n, lax.rem(at, n))
+            return carry
+        lax.fori_loop(1, 2 * n, step, 0)
+
+    def pack(values):
+        packed = jnp.zeros((rows, LANES), F32)
+        for i, value in enumerate(values):
+            packed = jnp.where(lane == i, value, packed)
+        return packed.T[:8]
+
+    def unpack(packed):
+        return jnp.concatenate([packed, jnp.zeros((LANES - 8, rows), F32)], axis=0).T
+
+    def own_tokens():
+        response = lax.broadcasted_iota(jnp.int32, (1, count), 1)
+        group = count // survive.shape[1]
+        kept = jnp.zeros((1, count), F32)
+        for g in range(survive.shape[1]):
+            inside = (response >= g * group) & (response < (g + 1) * group)
+            kept = jnp.where(inside, survive[0:1, g:g + 1].astype(F32), kept)
+        held = jnp.sum(kept * lengths[...].astype(F32), axis=1, keepdims=True)
+        tok[...] = jnp.broadcast_to(held, (8, LANES))
+        others(lambda b: send("tk", b, j, tok, tk.at[j], {"dp": b}))
+        tk[j] = tok[...]
+
+    def tokens():
+        others(lambda b: got("tk", b, tk.at[b]))
+        total = tk[0]
+        for b in range(1, n):
+            total = total + tk[b]
+        return 1.0 / total[0:1, 0:1]
+
+    def row_info():
+        row = lax.broadcasted_iota(jnp.int32, (rows, count), 0)
+        first = lax.broadcasted_iota(jnp.int32, (rows, count), 1) * positions
+        mine = (row >= first) & (row < first + positions)
+
+        def by_response(values):
+            return jnp.sum(jnp.where(mine, values, 0.0), axis=1, keepdims=True)
+
+        def by_position(values):
+            return by_response(jnp.concatenate([values] * count, axis=0))
+
+        slots = assign[...]
+        starts = slots * positions
+        hit = (row >= starts) & (row < starts + positions)
+        listed = jnp.sum(jnp.where(hit, 1.0, 0.0), axis=1, keepdims=True)
+        start = by_response(first.astype(F32))
+        place = lax.broadcasted_iota(jnp.int32, (rows, 1), 0).astype(F32) - start
+        live = place < by_response(lengths[...].astype(F32))
+        adv = by_response(advantage[...])
+        q = by_position(gap[...])
+        clipped = ((adv > 0) & (q > clip_high)) | ((adv < 0) & (q < clip_low))
+        weight = jnp.where(clipped | (~live), 0.0, -loss_scale * adv * listed)
+        rinfo[...] = jnp.where(lane == 0, weight, jnp.where(lane == 1, by_position(base[...]), 0.0))
+
+    def local_copy(i, a, b):
+        return pltpu.make_async_copy(a, b, ls.at[i])
+
+    def reduce_step(q, d):
+        slot = q * n
+
+        def rightward():
+            r = j + d
+
+            @pl.when(j > 0)
+            def _():
+                got("rr", slot + r, rin.at[0, q, r])
+                part[q, r] = (part[q, r].astype(F32) + rin[0, q, r].astype(F32)).astype(BF)
+            send("rr", slot + r, slot + r, part.at[q, r], rin.at[0, q, r], right)
+
+        def leftward():
+            r = j - d
+
+            @pl.when(j < n - 1)
+            def _():
+                got("rl", slot + r, rin.at[1, q, r])
+                part[q, r] = (part[q, r].astype(F32) + rin[1, q, r].astype(F32)).astype(BF)
+            send("rl", slot + r, slot + r, part.at[q, r], rin.at[1, q, r], left)
+
+        pl.when(j + d < n)(rightward)
+        pl.when(j - d >= 0)(leftward)
+
+    def reduce_own(q):
+        slot = q * n + j
+
+        @pl.when(j > 0)
+        def _():
+            got("rr", slot, rin.at[0, q, j])
+            own[q] += rin[0, q, j].astype(F32)
+
+        @pl.when(j < n - 1)
+        def _():
+            got("rl", slot, rin.at[1, q, j])
+            own[q] += rin[1, q, j].astype(F32)
+
+    def reduce_sent(q):
+        for d in range(1, n):
+            pl.when(j + d < n)(lambda: sent("rr", q * n + j + d, part.at[q, j + d]))
+            pl.when(j - d >= 0)(lambda: sent("rl", q * n + j - d, part.at[q, j - d]))
+
+    def gather_start(kind, at):
+        pl.when(j < n - 1)(lambda: send(kind, j, j, at(j), at(j), right))
+        pl.when(j > 0)(lambda: send(kind, n + j, j, at(j), at(j), left))
+
+    def gather_step(kind, at, d, fkind):
+        def pass_on(b, onward):
+            got(kind, b, at(b))
+            onward()
+            if fkind is not None:
+                send(fkind, b, b, at(b), at(b), partner)
+
+        def from_left():
+            b = j - d
+            pass_on(b, lambda: pl.when(j < n - 1)(lambda: send(kind, b, b, at(b), at(b), right)))
+
+        def from_right():
+            b = j + d
+            pass_on(b, lambda: pl.when(j > 0)(lambda: send(kind, n + b, b, at(b), at(b), left)))
+
+        pl.when(j - d >= 0)(from_left)
+        pl.when(j + d < n)(from_right)
+
+    def gather_sent(kind, at):
+        def one(b):
+            pl.when((b <= j) & (j < n - 1))(lambda: sent(kind, b, at(b)))
+            pl.when((b >= j) & (j > 0))(lambda: sent(kind, n + b, at(b)))
+        for b in range(n):
+            one(b)
+
+    def at_p0(b):
+        return p0.at[t, blk(b)]
+
+    def at_dp1(b):
+        return dp1.at[t, blk(b)]
+
+    def at_gz(b):
+        return gz.at[blk(b)]
+
+    def scalar_sums():
+        psr[j] = ps[j]
+        others(lambda b: got("ps", b, psr.at[b]))
+        sums = psr[0]
+        for b in range(1, n):
+            sums = sums + psr[b]
+        return unpack(sums)[:, 0:1]
+
+    def gram_send():
+        others(lambda b: send("mr", b, j, mp.at[b], mr.at[j], {"dp": b}))
+
+    def gram_reduce():
+        mr[j] = mp[j]
+        others(lambda b: got("mr", b, mr.at[b]))
+        total = mr[0].astype(F32)
+        for b in range(1, n):
+            total = total + mr[b].astype(F32)
+        mk[mrows(y, j)] = total.astype(BF)
+        replicas(lambda g, b: send(
+            "mk", g * n + b, y * n + j, mk.at[mrows(y, j)], mk.at[mrows(y, j)], {"groups": g, "dp": b}
+        ))
+
+    def gram_wait():
+        replicas(lambda g, b: got("mk", g * n + b, mk.at[mrows(g, b)]))
+
+    def store_gram(value):
+        value = value.astype(BF)
+        for b in range(n):
+            mp[b] = value[b * mb:(b + 1) * mb]
+
+    def main_start(src, other_src, main, other):
+        for d in range(n - 1, 0, -1):
+            at_distance(d, lambda b: send(
+                "a", b, j, src.at[:, wide(b, t)], main.at[blk(j), cols(t)], {"dp": b}
+            ))
+        local_copy(0, src.at[:, pl.ds(pl.multiple_of(j * chunk, chunk), chunk)], main.at[blk(j)]).start()
+        local_copy(1, other_src.at[:, pl.ds(pl.multiple_of(j * chunk, chunk), chunk)], other.at[blk(j)]).start()
+
+    def main_wait(src, other_src, main, other):
+        local_copy(0, src.at[:, pl.ds(0, chunk)], main.at[blk(j)]).wait()
+        local_copy(1, other_src.at[:, pl.ds(0, chunk)], other.at[blk(j)]).wait()
+
+    def main_arrive(main, d):
+        def first(b):
+            here = main.at[blk(b), cols(t)]
+            got("a", b, here)
+            send("ax", b, b, here, here, {"section": 1 - s})
+            send("af", b, b, here, here, partner)
+        at_distance(d, first)
+        at_distance(d, lambda b: got("af", b, main.at[blk(b), cols(o)]))
+
+    def other_arrive(other, d):
+        def first(b):
+            here = other.at[blk(b), cols(t)]
+            got("ax", b, here)
+            send("axf", b, b, here, here, partner)
+        at_distance(d, first)
+        at_distance(d, lambda b: got("axf", b, other.at[blk(b), cols(o)]))
+
+    barrier = pltpu.get_barrier_semaphore()
+
+    def greet(dev):
+        pl.semaphore_signal(barrier, inc=1, device_id=dev, device_id_type=pl.DeviceIdType.MESH)
+
+    def meet():
+        others(lambda b: greet({"dp": b}))
+
+        def across(b, carry):
+            greet({"groups": 1 - y, "dp": b})
+            return carry
+        lax.fori_loop(0, n, across, 0)
+        greet(partner)
+        greet({"section": 1 - s})
+        greet({"section": 1 - s, "tensor": o})
+        pl.semaphore_wait(barrier, 2 * n + 2)
+
+    def drain_common(main, other):
+        def one(b):
+            sent("a", b, main.at[blk(b), cols(t)])
+            sent("ax", b, main.at[blk(b), cols(t)])
+            sent("af", b, main.at[blk(b), cols(t)])
+            sent("axf", b, other.at[blk(b), cols(t)])
+            sent("mr", b, mp.at[b])
+            sent("ps", b, ps.at[b])
+            sent("tk", b, tk.at[b])
+            sent("g0f", b, at_p0(b))
+        others(one)
+        replicas(lambda g, b: sent("mk", g * n + b, mk.at[mrows(y, j)]))
+        sent("bf", 0, b0f.at[t])
+        gather_sent("g0", at_p0)
+        gather_sent("g1", at_dp1)
+        gather_sent("g2", at_gz)
+
+    def first_section():
+        local_copy(2, w1, wv1).start()
+        local_copy(3, w2, b0f.at[t]).start()
+        meet()
+        main_start(hid, une, xs, us)
+        send("bf", 0, 0, w2, b0f.at[t], partner)
+
+        @pl.when(t == y)
+        def _():
+            send("bx", 0, 0, w2, b0f.at[t], {"section": 1})
+        own_tokens()
+        local_copy(2, w1, wv1).wait()
+        local_copy(3, w2, b0f.at[t]).wait()
+        main_wait(hid, une, xs, us)
+
+        def project(b):
+            x = xs[blk(b)].astype(F32)
+            ps[b] = pack([jnp.sum(x * x, axis=1, keepdims=True)])
+            xg[blk(b)] = (x * gains[j]).astype(BF)
+            return dot(xg[blk(b)], wv1[...]), dot(xs[blk(b)], b0f[t], 1, 1)
+
+        def project_main(b):
+            pa, pb = project(b)
+            part[0, b] = pa.astype(BF)
+            part[1, b] = pb.astype(BF)
+            send("ps", b, j, ps.at[b], psr.at[j], {"dp": b})
+
+        def project_other(b):
+            part[2, b] = dot(us[blk(b)], b0f[t], 1, 1).astype(BF)
+
+        own[0], own[1] = project(j)
+        own[2] = dot(us[blk(j)], b0f[t], 1, 1)
+        got("bf", 0, b0f.at[o])
+        store_gram(dot(b0f[y], b0f[t], 1, 1))
+        gram_send()
+        for d in range(n - 1, 0, -1):
+            main_arrive(xs, d)
+            at_distance(d, project_main)
+
+        @pl.when(t != y)
+        def _():
+            send("bx", 0, 0, w2, b0f.at[t], {"section": 1})
+        gram_reduce()
+        for d in range(n - 1, 0, -1):
+            reduce_step(0, d)
+        reduce_own(0)
+        xx = scalar_sums()
+        inverse = lax.rsqrt(xx / width + eps_norm)
+        p0[t, blk(j)] = (inverse * own[0]).astype(BF)
+        send("p0", 0, t, at_p0(j), at_p0(j), partner)
+        for c in range(2):
+            send("p0", 1 + c, t, at_p0(j), at_p0(j), {"section": 1, "tensor": c})
+        gather_start("g0", at_p0)
+        for d in range(n - 1, 0, -1):
+            reduce_step(1, d)
+        for d in range(n - 1, 0, -1):
+            other_arrive(us, d)
+            at_distance(d, project_other)
+        for d in range(n - 1, 0, -1):
+            reduce_step(2, d)
+        reduce_own(1)
+        reduce_own(2)
+        gram_wait()
+        got("p0", o, p0.at[o, blk(j)])
+        kb = own[1] + dot(p0[0, blk(j)], mk[0:v]) + dot(p0[1, blk(j)], mk[v:2 * v])
+        p0v = p0[t, blk(j)].astype(F32)
+        scs[...] = pack([
+            xx,
+            jnp.sum(p0v * (own[1] + kb), axis=1, keepdims=True),
+            jnp.sum(p0v * own[2], axis=1, keepdims=True),
+        ])
+        for c in range(2):
+            send("s0", c, t, scs, scr.at[t], {"section": 1, "tensor": c})
+        own[1] = kb
+        for d in range(1, n):
+            gather_step("g0", at_p0, d, "g0f")
+        got("s1", 0, sc.at[j])
+        got("w", 0, wr.at[0])
+        got("w", 1, wr.at[1])
+        packed = unpack(sc[j])
+        seed, pull = packed[:, 0:1], packed[:, 1:2]
+        grad = seed * own[2] + wr[0].astype(F32) + wr[1].astype(F32) - pull * own[1]
+        gz[blk(j)] = (inverse * grad).astype(BF)
+        gather_start("g2", at_gz)
+        others(lambda b: send("gs", b, j, sc.at[j], sc.at[j], {"dp": b}))
+        got("d1", t, at_dp1(j))
+        gather_start("g1", at_dp1)
+        got("d1", o, dp1.at[o, blk(j)])
+        got("ax1", 0, a1f.at[t])
+        send("af1", 0, 0, a1f.at[t], a1f.at[t], partner)
+        got("gn", 0, gx)
+        scale = tokens()
+        for d in range(1, n):
+            gather_step("g2", at_gz, d, None)
+            gather_step("g1", at_dp1, d, "g1f")
+        others(lambda b: got("g0f", b, p0.at[o, blk(b)]))
+        others(lambda b: got("gs", b, sc.at[b]))
+        for b in range(n):
+            packed = unpack(sc[b])
+            for h in range(2):
+                gb[h, blk(b)] = (-packed[:, 1:2] * p0[h, blk(b)].astype(F32)).astype(BF)
+            ga[blk(b)] = (packed[:, 0:1] * p0[t, blk(b)].astype(F32)).astype(BF)
+        got("af1", 0, a1f.at[o])
+        others(lambda b: got("g1f", b, dp1.at[o, blk(b)]))
+        through = jnp.zeros((v, chunk), F32)
+        pulled = jnp.zeros((v, chunk), F32)
+        for h in range(2):
+            through += dot(dot(p0[t], dp1[h], 0, 0).astype(BF), a1f[h], 1, 1)
+            pulled += dot(dot(p0[t], gb[h], 0, 0).astype(BF), b0f[h])
+        total = gx[...] * through + pulled
+        total += dot(ga[...], us[...], 0, 0) + dot(gb[t], xs[...], 0, 0)
+        dw2[...] = total * scale
+        dw1[...] = dot(xg[...], gz[...], 0, 0) * scale
+        drain_common(xs, us)
+        sent("bx", 0, b0f.at[t])
+        sent("af1", 0, a1f.at[t])
+        for c in range(3):
+            sent("p0", c, at_p0(j))
+        for c in range(2):
+            sent("s0", c, scs)
+        others(lambda b: sent("gs", b, sc.at[b]))
+        others(lambda b: sent("g1f", b, at_dp1(b)))
+        for q in range(3):
+            reduce_sent(q)
+
+    def second_section():
+        local_copy(2, w1, a1f.at[t]).start()
+        local_copy(3, w2, wv2).start()
+        meet()
+        main_start(une, hid, us, xs)
+        own_tokens()
+        row_info()
+        local_copy(2, w1, a1f.at[t]).wait()
+        local_copy(3, w2, wv2).wait()
+        main_wait(une, hid, us, xs)
+
+        def project_main(b):
+            part[0, b] = dot(us[blk(b)], wv2[...], 1, 1).astype(BF)
+
+        def project(b):
+            x = xs[blk(b)].astype(F32)
+            ps[b] = pack([jnp.sum(x * us[blk(b)].astype(F32), axis=1, keepdims=True)])
+            xg[blk(b)] = (x * gains[j]).astype(BF)
+            return dot(xg[blk(b)], a1f[t])
+
+        def project_other(b):
+            part[1, b] = project(b).astype(BF)
+            send("ps", b, j, ps.at[b], psr.at[j], {"dp": b})
+
+        own[0] = dot(us[blk(j)], wv2[...], 1, 1)
+        own[1] = project(j)
+
+        def take_b0(mine):
+            @pl.when(mine)
+            def _():
+                got("bx", 0, b0f.at[t])
+                send("bf", 0, 0, b0f.at[t], b0f.at[t], partner)
+
+            @pl.when(~mine)
+            def _():
+                got("bf", 0, b0f.at[o])
+
+        for d in range(n - 1, 0, -1):
+            main_arrive(us, d)
+            at_distance(d, project_main)
+            if d == min(2, n - 1):
+                take_b0(t == y)
+                b0g[y] = (b0f[y].astype(F32) * gains[j]).astype(BF)
+                store_gram(dot(b0g[y], a1f[t]))
+                gram_send()
+        send("ax1", 0, 0, w1, a1f.at[t], {"section": 0})
+        send("gn", 0, 0, gains.at[j], gx, {"section": 0})
+        for d in range(n - 1, 0, -1):
+            reduce_step(0, d)
+        gram_reduce()
+        for d in range(n - 1, 0, -1):
+            other_arrive(xs, d)
+            at_distance(d, project_other)
+        for d in range(n - 1, 0, -1):
+            reduce_step(1, d)
+        reduce_own(0)
+        reduce_own(1)
+        dotted = scalar_sums()
+        gram_wait()
+        got("p0", 0, p0.at[0, blk(j)])
+        got("p0", 1, p0.at[1, blk(j)])
+        gather_start("g0", at_p0)
+        raised = own[1] + dot(p0[0, blk(j)], mk[0:v]) + dot(p0[1, blk(j)], mk[v:2 * v])
+        inn[...] = pack([jnp.sum(raised * own[0], axis=1, keepdims=True)])
+        send("in", 0, 0, inn, inr, partner)
+        got("s0", 0, scr.at[0])
+        got("s0", 1, scr.at[1])
+        got("in", 0, inr)
+        inner = unpack(inn[...] + inr[...])[:, 0:1]
+        sums = unpack(scr[0] + scr[1])
+        squares = 0.5 * sums[:, 0:1] + sums[:, 1:2]
+        inverse = lax.rsqrt(jnp.maximum(squares, 0.0) / width + eps_norm)
+        logit = dotted + sums[:, 2:3] + inverse * inner
+        weight = rinfo[:, 0:1]
+        seed = jnp.where(weight == 0.0, 0.0, weight * jnp.exp(logit - rinfo[:, 1:2]))
+        scaled = seed * inverse
+        dp1[t, blk(j)] = (scaled * own[0]).astype(BF)
+        back = dot(dp1[t, blk(j)], mk[...], 1, 1).astype(BF)
+        for c in range(2):
+            wsend[c] = back[:, c * v:(c + 1) * v]
+        scs[...] = pack([seed, inverse * inverse * inverse * (seed * inner) / width])
+        send("s1", 0, 0, scs, sc.at[j], {"section": 0})
+        for c in range(2):
+            send("w", c, t, wsend.at[c], wr.at[t], {"section": 0, "tensor": c})
+        for c in range(2):
+            send("d1", c, t, at_dp1(j), at_dp1(j), {"section": 0, "tensor": c})
+        gz[blk(j)] = (scaled * raised).astype(BF)
+        gather_start("g1", at_dp1)
+        gather_start("g2", at_gz)
+        take_b0(t != y)
+        for h in range(2):
+            b0g[h] = (b0f[h].astype(F32) * gains[j]).astype(BF)
+        scale = tokens()
+        for d in range(1, n):
+            gather_step("g0", at_p0, d, "g0f")
+        for d in range(1, n):
+            gather_step("g1", at_dp1, d, None)
+            gather_step("g2", at_gz, d, None)
+        others(lambda b: got("g0f", b, p0.at[o, blk(b)]))
+        dw2[...] = dot(gz[...], us[...], 0, 0) * scale
+        total = dot(xg[...], dp1[t], 0, 0)
+        for h in range(2):
+            total += dot(b0g[h], dot(p0[h], dp1[t], 0, 0).astype(BF), 0, 0)
+        dw1[...] = total * scale
+        drain_common(us, xs)
+        sent("ax1", 0, a1f.at[t])
+        sent("gn", 0, gx)
+        sent("in", 0, inn)
+        sent("s1", 0, scs)
+        for c in range(2):
+            sent("w", c, wsend.at[c])
+            sent("d1", c, at_dp1(j))
+        for q in range(2):
+            reduce_sent(q)
+
+    pl.when(s == 0)(first_section)
+    pl.when(s == 1)(second_section)
+
+
+def local_pair(
+    hidden, unembed, value_proj, output_proj, norm_gains, survive, lengths, assign,
+    advantage, reference_logit, recorded_gap,
+):
+    n = lax.axis_size("dp")
+    count, positions, width = hidden.shape
+    rows = count * positions
+    chunk, v = value_proj.shape[1:]
+    total = n * rows
+    kinds = len(PAIR_KINDS)
+    vm = pl.BlockSpec(memory_space=pltpu.VMEM)
+    hbm = pl.BlockSpec(memory_space=pl.ANY)
+    dw1, dw2 = pl.pallas_call(
+        functools.partial(pair_kernel, n, width),
+        out_shape=(
+            jax.ShapeDtypeStruct((chunk, v), F32),
+            jax.ShapeDtypeStruct((v, chunk), F32),
+        ),
+        in_specs=[hbm] * 4 + [vm] * 7,
+        out_specs=(vm, vm),
+        scratch_shapes=[
+            pltpu.VMEM((total, chunk), BF),
+            pltpu.VMEM((total, chunk), BF),
+            pltpu.VMEM((total, chunk), BF),
+            pltpu.VMEM((chunk, v), BF),
+            pltpu.VMEM((v, chunk), BF),
+            pltpu.VMEM((2, v, chunk), BF),
+            pltpu.VMEM((2, chunk, v), BF),
+            pltpu.VMEM((2, v, chunk), BF),
+            pltpu.VMEM((1, chunk), F32),
+            pltpu.VMEM((n, v // n, v), BF),
+            pltpu.VMEM((n, v // n, v), BF),
+            pltpu.VMEM((2 * v, v), BF),
+            pltpu.VMEM((3, n, rows, v), BF),
+            pltpu.VMEM((3, rows, v), F32),
+            pltpu.VMEM((2, 3, n, rows, v), BF),
+            pltpu.VMEM((2, total, v), BF),
+            pltpu.VMEM((2, total, v), BF),
+            pltpu.VMEM((total, v), BF),
+            pltpu.VMEM((total, v), BF),
+            pltpu.VMEM((2, total, v), BF),
+            pltpu.VMEM((2, rows, v), BF),
+            pltpu.VMEM((2, rows, v), BF),
+            pltpu.VMEM((n, 8, rows), F32),
+            pltpu.VMEM((n, 8, rows), F32),
+            pltpu.VMEM((8, rows), F32),
+            pltpu.VMEM((2, 8, rows), F32),
+            pltpu.VMEM((8, rows), F32),
+            pltpu.VMEM((8, rows), F32),
+            pltpu.VMEM((n, 8, rows), F32),
+            pltpu.VMEM((rows, LANES), F32),
+            pltpu.VMEM((8, LANES), F32),
+            pltpu.VMEM((n, 8, LANES), F32),
+            pltpu.SemaphoreType.DMA((kinds, 3 * n)),
+            pltpu.SemaphoreType.DMA((kinds, 3 * n)),
+            pltpu.SemaphoreType.DMA((4,)),
+        ],
+        compiler_params=pltpu.CompilerParams(
+            collective_id=0, has_side_effects=True, vmem_limit_bytes=60 * 1024 * 1024
+        ),
+    )(
+        hidden.reshape(rows, width), unembed.reshape(rows, width), value_proj[0], output_proj[0],
+        norm_gains[0].reshape(n, 1, chunk), survive.reshape(1, -1), lengths.reshape(1, count),
+        assign.reshape(1, count), advantage.reshape(1, count), reference_logit.T, recorded_gap.T,
+    )
+    return dw1[None], dw2[None]
+
+
 def solution(mesh):
     rowwise = P(("groups", "dp"))
     placed = (
@@ -514,8 +1132,10 @@
         P(("groups", "dp"), None),
         P(("groups", "dp"), None),
     )
+    shape = mesh.shape
+    paired = shape["section"] == 2 and shape["tensor"] == 2 and shape["groups"] == 2
     return jax.shard_map(
-        local,
+        local_pair if paired else local_chain,
         mesh=mesh,
         in_specs=placed,
         out_specs=(

time: 100 us -> 94.7 us (0.947)
  local copies, waits for them, and re-layouts: 7.6 us -> 3.62 us
  Pallas kernels: 91.1 us -> 89.2 us
    pallas_call x1, Pallas kernels: 91.1 us -> 89.2 us  [local_pair(): pl.pallas_call(functools.partial(pair_kernel, n, width), out_shape=(jax.S...]
    unnamed x10 -> x4, local copies, waits for them, and re-layouts: 5.31 us -> 3.62 us
    reshape x1 -> x0, local copies, waits for them, and re-layouts: 1.22 us -> none  [local(): jnp.where(s == sections - 1, unembed, hidden).reshape(rows, n * 2, half)]
    another operation x1 -> x0, local copies, waits for them, and re-layouts: 1.08 us -> none  [local(): w2 = output_proj[0].reshape(v, 2, half).transpose(1, 0, 2)]
where the time goes in v1:
time: 94.7 us; the launch traced here: 94.1 us
  Pallas kernels  89.2 us (94%)
  local copies, waits for them, and re-layouts  3.62 us (4%)
  between operations  1.3 us (1%)
    pallas_call x1, Pallas kernels, local_pair(): pl.pallas_call(functools.partial(pair_kernel, n, width), out_shape=(jax.S...  89.2 us
    unnamed x4, local copies, waits for them, and re-layouts  3.62 us

profile of v1, /device:TPU:0, one launch (start us, length us, event | category | flops | bytes accessed | tf_op | source)
XLA Modules:
  0.0 94.1 jit_solution(2380061694936718293)
XLA Ops:
  1.3 89.2 %shard_map.122 = (f32[1280,256]{1,0:T(8,128)}, f32[256,1280]{1,0:T(8,128)}) custom-call(bf16[128,5120]{1,0:T(8,128)(2,1)} %bitcast.14, bf16[128,5120]{1,0:T(8,128)(2,1)} %bitcast.15, bf16[1280,256]{1,0:T(8,128)(2,1)} %bitcast.18, bf16[256,1280]{1,0:T(8,128)(2,1)} %bitcast.19, f32[4,1,1280]{2,1,0:T(1,128)} %bitcast.20, s32[1,1]{1,0:T(1,128)} %bitcast.13.survive, ...), custom_call_target="tpu_custom_call" | custom-call | tf_op jit(solution)/shard_map/pallas_call | solution.py:1064
  90.5 0.0 copy-start
  90.5 2.6 %copy.16 = f32[1,1280,256]{2,1,0:T(8,128)} copy(f32[1,1280,256]{2,1,0:T(8,128)} %bitcast.17) | data formatting | bytes 2621440
  93.1 0.0 copy-done
  93.1 1.1 %copy.17 = f32[1,256,1280]{2,1,0:T(8,128)} copy(f32[1,256,1280]{2,1,0:T(8,128)S(1)} %bitcast.16) | data formatting | bytes 2621440
Async XLA Ops:
  90.5 2.6 %copy-start = (f32[256,1280]{1,0:T(8,128)S(1)}, f32[256,1280]{1,0:T(8,128)}, u32[]{:S(2)}) copy-start(f32[256,1280]{1,0:T(8,128)} %get-tuple-element.5) | copy-start | bytes 3932164

commit v2 on v1

--- a/solution.py
+++ b/solution.py
@@ -499,17 +499,24 @@
     )
 
 
-PAIR_KINDS = (
-    "a", "af", "ax", "axf", "bx", "bf", "ax1", "af1", "gn", "mr", "mk", "rr", "rl", "ps", "p0", "s0",
-    "in", "w", "d1", "s1", "g0", "g0f", "g1", "g1f", "g2", "gs", "tk",
-)
+def pair_slots(n):
+    sizes = {
+        "a": n, "af": n, "ax": n, "axf": n, "bx": 1, "bf": 1, "by": 1, "ax1": 1, "af1": 1, "ay": 1, "gn": 1,
+        "mr": n, "mk": n, "my": n, "rr": 3 * n, "rl": 3 * n, "ps": n, "p0": 3, "s0": 2, "in": 1, "w": 2,
+        "d1": 2, "s1": 1, "g0": n, "g0x": n, "g0f": n, "g1": n, "gx": n, "g1f": n, "g2": n, "gs": n, "tk": n,
+    }
+    starts, total = {}, 0
+    for kind, size in sizes.items():
+        starts[kind] = total
+        total += size
+    return starts, total
 
 
 def pair_kernel(
     n, width,
     hid, une, w1, w2, gains, survive, lengths, assign, advantage, base, gap,
-    dw1, dw2,
-    xs, us, xg, wv1, wv2, b0f, a1f, b0g, gx, mp, mr, mk, part, own, rin, p0, dp1, gz, ga, gb,
+    dw1_out, dw2_out,
+    dw1, dw2, xs, us, xg, wv1, wv2, b0f, a1f, b0g, gx, mp, mr, mk, part, own, rin, p0, dp1, gz, ga, gb, gc,
     wr, wsend, ps, psr, scs, scr, inn, inr, sc, rinfo, tok, tk,
     ss, rs, ls,
 ):
@@ -527,6 +534,7 @@
     right = {"dp": j + 1}
     left = {"dp": j - 1}
     lane = lax.broadcasted_iota(jnp.int32, (rows, LANES), 1)
+    starts, _ = pair_slots(n)
 
     def blk(b):
         return pl.ds(pl.multiple_of(b * rows, rows), rows)
@@ -541,16 +549,16 @@
         return pl.ds(pl.multiple_of(g * v + b * mb, mb), mb)
 
     def send(kind, si, ri, a, b, dev):
-        k = PAIR_KINDS.index(kind)
+        k = starts[kind]
         pltpu.make_async_remote_copy(
-            src_ref=a, dst_ref=b, send_sem=ss.at[k, si], recv_sem=rs.at[k, ri],
+            src_ref=a, dst_ref=b, send_sem=ss.at[k + si], recv_sem=rs.at[k + ri],
             device_id=dev, device_id_type=pl.DeviceIdType.MESH,
         ).start()
 
     def handle(kind, i, a):
-        k = PAIR_KINDS.index(kind)
+        k = starts[kind]
         return pltpu.make_async_remote_copy(
-            src_ref=a, dst_ref=a, send_sem=ss.at[k, i], recv_sem=rs.at[k, i],
+            src_ref=a, dst_ref=a, send_sem=ss.at[k + i], recv_sem=rs.at[k + i],
             device_id=partner, device_id_type=pl.DeviceIdType.MESH,
         )
 
@@ -569,13 +577,6 @@
     def at_distance(d, body):
         pl.when(j + d < n)(lambda: body(j + d))
         pl.when(j - d >= 0)(lambda: body(j - d))
-
-    def replicas(body):
-        def step(k, carry):
-            at = lax.rem(y * n + j + k, 2 * n)
-            body(at // n, lax.rem(at, n))
-            return carry
-        lax.fori_loop(1, 2 * n, step, 0)
 
     def pack(values):
         packed = jnp.zeros((rows, LANES), F32)
@@ -632,29 +633,23 @@
     def local_copy(i, a, b):
         return pltpu.make_async_copy(a, b, ls.at[i])
 
-    def reduce_step(q, d):
+    def reduce_step(q, d, at_end):
         slot = q * n
 
-        def rightward():
-            r = j + d
-
-            @pl.when(j > 0)
-            def _():
-                got("rr", slot + r, rin.at[0, q, r])
-                part[q, r] = (part[q, r].astype(F32) + rin[0, q, r].astype(F32)).astype(BF)
-            send("rr", slot + r, slot + r, part.at[q, r], rin.at[0, q, r], right)
-
-        def leftward():
-            r = j - d
-
-            @pl.when(j < n - 1)
-            def _():
-                got("rl", slot + r, rin.at[1, q, r])
-                part[q, r] = (part[q, r].astype(F32) + rin[1, q, r].astype(F32)).astype(BF)
-            send("rl", slot + r, slot + r, part.at[q, r], rin.at[1, q, r], left)
-
-        pl.when(j + d < n)(rightward)
-        pl.when(j - d >= 0)(leftward)
+        def onward(kind, way, r, dev):
+            if not at_end:
+                got(kind, slot + r, rin.at[way, q, r])
+                part[q, r] = (part[q, r].astype(F32) + rin[way, q, r].astype(F32)).astype(BF)
+            send(kind, slot + r, slot + r, part.at[q, r], rin.at[way, q, r], dev)
+
+        first = j == 0 if at_end else (j > 0) & (j + d < n)
+        final = j == n - 1 if at_end else (j < n - 1) & (j - d >= 0)
+        pl.when(first)(lambda: onward("rr", 0, j + d, right))
+        pl.when(final)(lambda: onward("rl", 1, j - d, left))
+
+    def reduce_inner(q, most, least=1):
+        for d in range(most, least - 1, -1):
+            reduce_step(q, d, False)
 
     def reduce_own(q):
         slot = q * n + j
@@ -674,34 +669,9 @@
             pl.when(j + d < n)(lambda: sent("rr", q * n + j + d, part.at[q, j + d]))
             pl.when(j - d >= 0)(lambda: sent("rl", q * n + j - d, part.at[q, j - d]))
 
-    def gather_start(kind, at):
-        pl.when(j < n - 1)(lambda: send(kind, j, j, at(j), at(j), right))
-        pl.when(j > 0)(lambda: send(kind, n + j, j, at(j), at(j), left))
-
-    def gather_step(kind, at, d, fkind):
-        def pass_on(b, onward):
-            got(kind, b, at(b))
-            onward()
-            if fkind is not None:
-                send(fkind, b, b, at(b), at(b), partner)
-
-        def from_left():
-            b = j - d
-            pass_on(b, lambda: pl.when(j < n - 1)(lambda: send(kind, b, b, at(b), at(b), right)))
-
-        def from_right():
-            b = j + d
-            pass_on(b, lambda: pl.when(j > 0)(lambda: send(kind, n + b, b, at(b), at(b), left)))
-
-        pl.when(j - d >= 0)(from_left)
-        pl.when(j + d < n)(from_right)
-
-    def gather_sent(kind, at):
-        def one(b):
-            pl.when((b <= j) & (j < n - 1))(lambda: sent(kind, b, at(b)))
-            pl.when((b >= j) & (j > 0))(lambda: sent(kind, n + b, at(b)))
-        for b in range(n):
-            one(b)
+    def gather(kind, at):
+        for d in range(n - 1, 0, -1):
+            at_distance(d, lambda b: send(kind, b, j, at(j), at(j), {"dp": b}))
 
     def at_p0(b):
         return p0.at[t, blk(b)]
@@ -730,23 +700,34 @@
         for b in range(1, n):
             total = total + mr[b].astype(F32)
         mk[mrows(y, j)] = total.astype(BF)
-        replicas(lambda g, b: send(
-            "mk", g * n + b, y * n + j, mk.at[mrows(y, j)], mk.at[mrows(y, j)], {"groups": g, "dp": b}
-        ))
+        here = mk.at[mrows(y, j)]
+        others(lambda b: send("mk", b, j, here, here, {"dp": b}))
+        send("my", j, j, here, here, {"groups": 1 - y})
+
+    def gram_pass():
+        def across(b):
+            here = mk.at[mrows(y, b)]
+            got("mk", b, here)
+            send("my", b, b, here, here, {"groups": 1 - y})
+        others(across)
 
     def gram_wait():
-        replicas(lambda g, b: got("mk", g * n + b, mk.at[mrows(g, b)]))
+        for b in range(n):
+            got("my", b, mk.at[mrows(1 - y, b)])
 
     def store_gram(value):
         value = value.astype(BF)
         for b in range(n):
             mp[b] = value[b * mb:(b + 1) * mb]
 
+    def main_send(src, main, d):
+        at_distance(d, lambda b: send(
+            "a", b, j, src.at[:, wide(b, t)], main.at[blk(j), cols(t)], {"dp": b}
+        ))
+
     def main_start(src, other_src, main, other):
-        for d in range(n - 1, 0, -1):
-            at_distance(d, lambda b: send(
-                "a", b, j, src.at[:, wide(b, t)], main.at[blk(j), cols(t)], {"dp": b}
-            ))
+        for d in range(n - 1, 1, -1):
+            main_send(src, main, d)
         local_copy(0, src.at[:, pl.ds(pl.multiple_of(j * chunk, chunk), chunk)], main.at[blk(j)]).start()
         local_copy(1, other_src.at[:, pl.ds(pl.multiple_of(j * chunk, chunk), chunk)], other.at[blk(j)]).start()
 
@@ -778,15 +759,11 @@
 
     def meet():
         others(lambda b: greet({"dp": b}))
-
-        def across(b, carry):
-            greet({"groups": 1 - y, "dp": b})
-            return carry
-        lax.fori_loop(0, n, across, 0)
+        greet({"groups": 1 - y})
         greet(partner)
         greet({"section": 1 - s})
         greet({"section": 1 - s, "tensor": o})
-        pl.semaphore_wait(barrier, 2 * n + 2)
+        pl.semaphore_wait(barrier, n + 3)
 
     def drain_common(main, other):
         def one(b):
@@ -798,23 +775,23 @@
             sent("ps", b, ps.at[b])
             sent("tk", b, tk.at[b])
             sent("g0f", b, at_p0(b))
+            sent("g2", b, at_gz(b))
+            sent("gs", b, sc.at[b])
         others(one)
-        replicas(lambda g, b: sent("mk", g * n + b, mk.at[mrows(y, j)]))
+        others(lambda b: sent("mk", b, mk.at[mrows(y, j)]))
+        for b in range(n):
+            sent("my", b, mk.at[mrows(y, b)])
         sent("bf", 0, b0f.at[t])
-        gather_sent("g0", at_p0)
-        gather_sent("g1", at_dp1)
-        gather_sent("g2", at_gz)
 
     def first_section():
         local_copy(2, w1, wv1).start()
         local_copy(3, w2, b0f.at[t]).start()
         meet()
-        main_start(hid, une, xs, us)
-        send("bf", 0, 0, w2, b0f.at[t], partner)
-
         @pl.when(t == y)
         def _():
             send("bx", 0, 0, w2, b0f.at[t], {"section": 1})
+        main_start(hid, une, xs, us)
+        send("bf", 0, 0, w2, b0f.at[t], partner)
         own_tokens()
         local_copy(2, w1, wv1).wait()
         local_copy(3, w2, b0f.at[t]).wait()
@@ -840,16 +817,20 @@
         got("bf", 0, b0f.at[o])
         store_gram(dot(b0f[y], b0f[t], 1, 1))
         gram_send()
+        main_send(hid, xs, 1)
         for d in range(n - 1, 0, -1):
             main_arrive(xs, d)
             at_distance(d, project_main)
-
-        @pl.when(t != y)
-        def _():
-            send("bx", 0, 0, w2, b0f.at[t], {"section": 1})
+            reduce_step(0, d, True)
+            reduce_step(1, d, True)
+        reduce_inner(0, n - 2)
+        reduce_inner(1, n - 2, 2)
         gram_reduce()
         for d in range(n - 1, 0, -1):
-            reduce_step(0, d)
+            other_arrive(us, d)
+            at_distance(d, project_other)
+            reduce_step(2, d, True)
+        reduce_inner(1, 1)
         reduce_own(0)
         xx = scalar_sums()
         inverse = lax.rsqrt(xx / width + eps_norm)
@@ -857,14 +838,15 @@
         send("p0", 0, t, at_p0(j), at_p0(j), partner)
         for c in range(2):
             send("p0", 1 + c, t, at_p0(j), at_p0(j), {"section": 1, "tensor": c})
-        gather_start("g0", at_p0)
-        for d in range(n - 1, 0, -1):
-            reduce_step(1, d)
-        for d in range(n - 1, 0, -1):
-            other_arrive(us, d)
-            at_distance(d, project_other)
-        for d in range(n - 1, 0, -1):
-            reduce_step(2, d)
+        reduce_inner(2, n - 2, 2)
+        gram_pass()
+        reduce_inner(2, 1)
+
+        @pl.when(t == y)
+        def _():
+            got("ax1", 0, a1f.at[t])
+            send("ay", 0, 0, a1f.at[t], a1f.at[t], {"groups": 1 - y})
+            send("af1", 0, 0, a1f.at[t], a1f.at[t], partner)
         reduce_own(1)
         reduce_own(2)
         gram_wait()
@@ -878,57 +860,77 @@
         ])
         for c in range(2):
             send("s0", c, t, scs, scr.at[t], {"section": 1, "tensor": c})
+        gather("g0", at_p0)
         own[1] = kb
-        for d in range(1, n):
-            gather_step("g0", at_p0, d, "g0f")
-        got("s1", 0, sc.at[j])
         got("w", 0, wr.at[0])
         got("w", 1, wr.at[1])
+        got("s1", 0, sc.at[j])
+        others(lambda b: send("gs", b, j, sc.at[j], sc.at[j], {"dp": b}))
         packed = unpack(sc[j])
-        seed, pull = packed[:, 0:1], packed[:, 1:2]
-        grad = seed * own[2] + wr[0].astype(F32) + wr[1].astype(F32) - pull * own[1]
+        grad = packed[:, 0:1] * own[2] - packed[:, 2:3] * own[1]
+        grad += packed[:, 1:2] * (wr[0].astype(F32) + wr[1].astype(F32))
         gz[blk(j)] = (inverse * grad).astype(BF)
-        gather_start("g2", at_gz)
-        others(lambda b: send("gs", b, j, sc.at[j], sc.at[j], {"dp": b}))
-        got("d1", t, at_dp1(j))
-        gather_start("g1", at_dp1)
-        got("d1", o, dp1.at[o, blk(j)])
-        got("ax1", 0, a1f.at[t])
-        send("af1", 0, 0, a1f.at[t], a1f.at[t], partner)
+        gather("g2", at_gz)
+
+        def pass_p0(b):
+            got("g0", b, at_p0(b))
+            send("g0f", b, b, at_p0(b), at_p0(b), partner)
+            send("g0x", b, b, at_p0(b), at_p0(b), {"section": 1})
+        others(pass_p0)
+
+        @pl.when(t != y)
+        def _():
+            got("ay", 0, a1f.at[t])
+            send("af1", 0, 0, a1f.at[t], a1f.at[t], partner)
         got("gn", 0, gx)
         scale = tokens()
-        for d in range(1, n):
-            gather_step("g2", at_gz, d, None)
-            gather_step("g1", at_dp1, d, "g1f")
+
+        def pass_dp1(b):
+            got("gx", b, at_dp1(b))
+            send("g1f", b, b, at_dp1(b), at_dp1(b), partner)
+        others(pass_dp1)
         others(lambda b: got("g0f", b, p0.at[o, blk(b)]))
+        got("d1", t, at_dp1(j))
+        got("d1", o, dp1.at[o, blk(j)])
+        got("af1", 0, a1f.at[o])
+        others(lambda b: got("g1f", b, dp1.at[o, blk(b)]))
         others(lambda b: got("gs", b, sc.at[b]))
         for b in range(n):
             packed = unpack(sc[b])
+            held = p0[t, blk(b)].astype(F32)
             for h in range(2):
-                gb[h, blk(b)] = (-packed[:, 1:2] * p0[h, blk(b)].astype(F32)).astype(BF)
-            ga[blk(b)] = (packed[:, 0:1] * p0[t, blk(b)].astype(F32)).astype(BF)
-        got("af1", 0, a1f.at[o])
-        others(lambda b: got("g1f", b, dp1.at[o, blk(b)]))
+                gb[h, blk(b)] = (-packed[:, 2:3] * p0[h, blk(b)].astype(F32)).astype(BF)
+            ga[blk(b)] = (packed[:, 0:1] * held).astype(BF)
+            gc[blk(b)] = (packed[:, 1:2] * held).astype(BF)
         through = jnp.zeros((v, chunk), F32)
-        pulled = jnp.zeros((v, chunk), F32)
         for h in range(2):
-            through += dot(dot(p0[t], dp1[h], 0, 0).astype(BF), a1f[h], 1, 1)
-            pulled += dot(dot(p0[t], gb[h], 0, 0).astype(BF), b0f[h])
-        total = gx[...] * through + pulled
-        total += dot(ga[...], us[...], 0, 0) + dot(gb[t], xs[...], 0, 0)
-        dw2[...] = total * scale
+            through += dot(dot(gc[...], dp1[h], 0, 0).astype(BF), a1f[h], 1, 1)
+        dw2[...] = gx[...] * through
+        for h in range(2):
+            dw2[...] += dot(dot(p0[t], gb[h], 0, 0).astype(BF), b0f[h])
+        dw2[...] = (dw2[...] + dot(ga[...], us[...], 0, 0) + dot(gb[t], xs[...], 0, 0)) * scale
+        local_copy(1, dw2, dw2_out).start()
+        others(lambda b: got("g2", b, at_gz(b)))
         dw1[...] = dot(xg[...], gz[...], 0, 0) * scale
+        local_copy(0, dw1, dw1_out).start()
         drain_common(xs, us)
-        sent("bx", 0, b0f.at[t])
+
+        @pl.when(t == y)
+        def _():
+            sent("bx", 0, b0f.at[t])
+            sent("ay", 0, a1f.at[t])
         sent("af1", 0, a1f.at[t])
         for c in range(3):
             sent("p0", c, at_p0(j))
         for c in range(2):
             sent("s0", c, scs)
-        others(lambda b: sent("gs", b, sc.at[b]))
+        others(lambda b: sent("g0", b, at_p0(b)))
+        others(lambda b: sent("g0x", b, at_p0(b)))
         others(lambda b: sent("g1f", b, at_dp1(b)))
         for q in range(3):
             reduce_sent(q)
+        local_copy(0, dw1, dw1_out).wait()
+        local_copy(1, dw2, dw2_out).wait()
 
     def second_section():
         local_copy(2, w1, a1f.at[t]).start()
@@ -956,48 +958,72 @@
 
         own[0] = dot(us[blk(j)], wv2[...], 1, 1)
         own[1] = project(j)
-
-        def take_b0(mine):
-            @pl.when(mine)
+        main_send(une, us, 1)
+
+        def take_b0():
+            @pl.when(t == y)
             def _():
                 got("bx", 0, b0f.at[t])
                 send("bf", 0, 0, b0f.at[t], b0f.at[t], partner)
-
-            @pl.when(~mine)
+                send("by", 0, 0, b0f.at[t], b0f.at[t], {"groups": 1 - y})
+
+            @pl.when(t != y)
+            def _():
+                got("bf", 0, b0f.at[o])
+
+        def take_rest():
+            @pl.when(t != y)
+            def _():
+                got("by", 0, b0f.at[t])
+                send("bf", 0, 0, b0f.at[t], b0f.at[t], partner)
+
+            @pl.when(t == y)
             def _():
                 got("bf", 0, b0f.at[o])
 
         for d in range(n - 1, 0, -1):
             main_arrive(us, d)
             at_distance(d, project_main)
+            reduce_step(0, d, True)
             if d == min(2, n - 1):
-                take_b0(t == y)
+                take_b0()
                 b0g[y] = (b0f[y].astype(F32) * gains[j]).astype(BF)
                 store_gram(dot(b0g[y], a1f[t]))
                 gram_send()
-        send("ax1", 0, 0, w1, a1f.at[t], {"section": 0})
+        @pl.when(t == y)
+        def _():
+            send("ax1", 0, 0, w1, a1f.at[t], {"section": 0})
         send("gn", 0, 0, gains.at[j], gx, {"section": 0})
-        for d in range(n - 1, 0, -1):
-            reduce_step(0, d)
+        reduce_inner(0, n - 2)
         gram_reduce()
         for d in range(n - 1, 0, -1):
             other_arrive(xs, d)
             at_distance(d, project_other)
-        for d in range(n - 1, 0, -1):
-            reduce_step(1, d)
+            reduce_step(1, d, True)
+        reduce_inner(1, n - 2)
         reduce_own(0)
+        dp1[t, blk(j)] = own[0].astype(BF)
+        for c in range(2):
+            send("d1", c, t, at_dp1(j), at_dp1(j), {"section": 0, "tensor": c})
+        gram_pass()
+        gram_wait()
+        back = dot(dp1[t, blk(j)], mk[...], 1, 1).astype(BF)
+        for c in range(2):
+            wsend[c] = back[:, c * v:(c + 1) * v]
+            send("w", c, t, wsend.at[c], wr.at[t], {"section": 0, "tensor": c})
         reduce_own(1)
         dotted = scalar_sums()
-        gram_wait()
+        gather("g1", at_dp1)
         got("p0", 0, p0.at[0, blk(j)])
         got("p0", 1, p0.at[1, blk(j)])
-        gather_start("g0", at_p0)
         raised = own[1] + dot(p0[0, blk(j)], mk[0:v]) + dot(p0[1, blk(j)], mk[v:2 * v])
         inn[...] = pack([jnp.sum(raised * own[0], axis=1, keepdims=True)])
         send("in", 0, 0, inn, inr, partner)
+        gz[blk(j)] = raised.astype(BF)
+        gather("g2", at_gz)
+        got("in", 0, inr)
         got("s0", 0, scr.at[0])
         got("s0", 1, scr.at[1])
-        got("in", 0, inr)
         inner = unpack(inn[...] + inr[...])[:, 0:1]
         sums = unpack(scr[0] + scr[1])
         squares = 0.5 * sums[:, 0:1] + sums[:, 1:2]
@@ -1006,44 +1032,55 @@
         weight = rinfo[:, 0:1]
         seed = jnp.where(weight == 0.0, 0.0, weight * jnp.exp(logit - rinfo[:, 1:2]))
         scaled = seed * inverse
-        dp1[t, blk(j)] = (scaled * own[0]).astype(BF)
-        back = dot(dp1[t, blk(j)], mk[...], 1, 1).astype(BF)
-        for c in range(2):
-            wsend[c] = back[:, c * v:(c + 1) * v]
-        scs[...] = pack([seed, inverse * inverse * inverse * (seed * inner) / width])
-        send("s1", 0, 0, scs, sc.at[j], {"section": 0})
-        for c in range(2):
-            send("w", c, t, wsend.at[c], wr.at[t], {"section": 0, "tensor": c})
-        for c in range(2):
-            send("d1", c, t, at_dp1(j), at_dp1(j), {"section": 0, "tensor": c})
-        gz[blk(j)] = (scaled * raised).astype(BF)
-        gather_start("g1", at_dp1)
-        gather_start("g2", at_gz)
-        take_b0(t != y)
+        sc[j] = pack([seed, scaled, inverse * inverse * inverse * (seed * inner) / width])
+        send("s1", 0, 0, sc.at[j], sc.at[j], {"section": 0})
+        others(lambda b: send("gs", b, j, sc.at[j], sc.at[j], {"dp": b}))
+
+        def pass_dp1(b):
+            got("g1", b, at_dp1(b))
+            send("gx", b, b, at_dp1(b), at_dp1(b), {"section": 0})
+        others(pass_dp1)
+        take_rest()
         for h in range(2):
             b0g[h] = (b0f[h].astype(F32) * gains[j]).astype(BF)
         scale = tokens()
-        for d in range(1, n):
-            gather_step("g0", at_p0, d, "g0f")
-        for d in range(1, n):
-            gather_step("g1", at_dp1, d, None)
-            gather_step("g2", at_gz, d, None)
+
+        def pass_p0(b):
+            got("g0x", b, at_p0(b))
+            send("g0f", b, b, at_p0(b), at_p0(b), partner)
+        others(pass_p0)
         others(lambda b: got("g0f", b, p0.at[o, blk(b)]))
-        dw2[...] = dot(gz[...], us[...], 0, 0) * scale
-        total = dot(xg[...], dp1[t], 0, 0)
+        others(lambda b: got("g2", b, at_gz(b)))
+        others(lambda b: got("gs", b, sc.at[b]))
+        for b in range(n):
+            scaled = unpack(sc[b])[:, 1:2]
+            ga[blk(b)] = (scaled * gz[blk(b)].astype(F32)).astype(BF)
+            gc[blk(b)] = (scaled * dp1[t, blk(b)].astype(F32)).astype(BF)
+        dw2[...] = dot(ga[...], us[...], 0, 0) * scale
+        local_copy(1, dw2, dw2_out).start()
+        total = dot(xg[...], gc[...], 0, 0)
         for h in range(2):
-            total += dot(b0g[h], dot(p0[h], dp1[t], 0, 0).astype(BF), 0, 0)
+            total += dot(b0g[h], dot(p0[h], gc[...], 0, 0).astype(BF), 0, 0)
         dw1[...] = total * scale
+        local_copy(0, dw1, dw1_out).start()
         drain_common(us, xs)
-        sent("ax1", 0, a1f.at[t])
+
+        @pl.when(t == y)
+        def _():
+            sent("ax1", 0, a1f.at[t])
+            sent("by", 0, b0f.at[t])
         sent("gn", 0, gx)
+        others(lambda b: sent("g1", b, at_dp1(b)))
+        others(lambda b: sent("gx", b, at_dp1(b)))
         sent("in", 0, inn)
-        sent("s1", 0, scs)
+        sent("s1", 0, sc.at[j])
         for c in range(2):
             sent("w", c, wsend.at[c])
             sent("d1", c, at_dp1(j))
         for q in range(2):
             reduce_sent(q)
+        local_copy(0, dw1, dw1_out).wait()
+        local_copy(1, dw2, dw2_out).wait()
 
     pl.when(s == 0)(first_section)
     pl.when(s == 1)(second_section)
@@ -1058,7 +1095,7 @@
     rows = count * positions
     chunk, v = value_proj.shape[1:]
     total = n * rows
-    kinds = len(PAIR_KINDS)
+    _, slots = pair_slots(n)
     vm = pl.BlockSpec(memory_space=pltpu.VMEM)
     hbm = pl.BlockSpec(memory_space=pl.ANY)
     dw1, dw2 = pl.pallas_call(
@@ -1068,8 +1105,10 @@
             jax.ShapeDtypeStruct((v, chunk), F32),
         ),
         in_specs=[hbm] * 4 + [vm] * 7,
-        out_specs=(vm, vm),
+        out_specs=(hbm, hbm),
         scratch_shapes=[
+            pltpu.VMEM((chunk, v), F32),
+            pltpu.VMEM((v, chunk), F32),
             pltpu.VMEM((total, chunk), BF),
             pltpu.VMEM((total, chunk), BF),
             pltpu.VMEM((total, chunk), BF),
@@ -1090,6 +1129,7 @@
             pltpu.VMEM((total, v), BF),
             pltpu.VMEM((total, v), BF),
             pltpu.VMEM((2, total, v), BF),
+            pltpu.VMEM((total, v), BF),
             pltpu.VMEM((2, rows, v), BF),
             pltpu.VMEM((2, rows, v), BF),
             pltpu.VMEM((n, 8, rows), F32),
@@ -1102,8 +1142,8 @@
             pltpu.VMEM((rows, LANES), F32),
             pltpu.VMEM((8, LANES), F32),
             pltpu.VMEM((n, 8, LANES), F32),
-            pltpu.SemaphoreType.DMA((kinds, 3 * n)),
-            pltpu.SemaphoreType.DMA((kinds, 3 * n)),
+            pltpu.SemaphoreType.DMA((slots,)),
+            pltpu.SemaphoreType.DMA((slots,)),
             pltpu.SemaphoreType.DMA((4,)),
         ],
         compiler_params=pltpu.CompilerParams(

time: 94.7 us -> 68.9 us (0.73)
  the two profiles are of different devices: /device:TPU:0 before, /device:TPU:9 now
where the time goes in v2:
time: 68.9 us; the launch traced here: 68.6 us
  Pallas kernels  63.7 us (92%)
  local copies, waits for them, and re-layouts  3.62 us (5%)
  between operations  1.3 us (2%)
    pallas_call x1, Pallas kernels, local_pair(): pl.pallas_call(functools.partial(pair_kernel, n, width), out_shape=(jax.S...  63.7 us
    unnamed x4, local copies, waits for them, and re-layouts  3.62 us

profile of v2, /device:TPU:9, one launch (start us, length us, event | category | flops | bytes accessed | tf_op | source)
XLA Modules:
  0.0 68.6 jit_solution(2993786222647752664)
XLA Ops:
  1.3 63.7 %shard_map.122 = (f32[1280,256]{1,0:T(8,128)}, f32[256,1280]{1,0:T(8,128)}) custom-call(bf16[128,5120]{1,0:T(8,128)(2,1)} %bitcast.14, bf16[128,5120]{1,0:T(8,128)(2,1)} %bitcast.15, bf16[1280,256]{1,0:T(8,128)(2,1)} %bitcast.18, bf16[256,1280]{1,0:T(8,128)(2,1)} %bitcast.19, f32[4,1,1280]{2,1,0:T(1,128)} %bitcast.20, s32[1,1]{1,0:T(1,128)} %bitcast.13.survive, ...), custom_call_target="tpu_custom_call" | custom-call | tf_op jit(solution)/shard_map/pallas_call | solution.py:1101
  65.0 0.0 copy-start
  65.0 2.6 %copy.16 = f32[1,1280,256]{2,1,0:T(8,128)} copy(f32[1,1280,256]{2,1,0:T(8,128)} %bitcast.17) | data formatting | bytes 2621440
  67.6 0.0 copy-done
  67.6 1.1 %copy.17 = f32[1,256,1280]{2,1,0:T(8,128)} copy(f32[1,256,1280]{2,1,0:T(8,128)S(1)} %bitcast.16) | data formatting | bytes 2621440
Async XLA Ops:
  65.0 2.6 %copy-start = (f32[256,1280]{1,0:T(8,128)S(1)}, f32[256,1280]{1,0:T(8,128)}, u32[]{:S(2)}) copy-start(f32[256,1280]{1,0:T(8,128)} %get-tuple-element.5) | copy-start | bytes 3932164

commit v3 on v2

--- a/solution.py
+++ b/solution.py
@@ -502,21 +502,21 @@
 def pair_slots(n):
     sizes = {
         "a": n, "af": n, "ax": n, "axf": n, "bx": 1, "bf": 1, "by": 1, "ax1": 1, "af1": 1, "ay": 1, "gn": 1,
-        "mr": n, "mk": n, "my": n, "rr": 3 * n, "rl": 3 * n, "ps": n, "p0": 3, "s0": 2, "in": 1, "w": 2,
+        "mr": n, "mk": n, "my": n, "rr": 3 * n, "rl": 3 * n, "ps": n, "p0": 2, "s0": 1, "in": 2, "w": 2,
         "d1": 2, "s1": 1, "g0": n, "g0x": n, "g0f": n, "g1": n, "gx": n, "g1f": n, "g2": n, "gs": n, "tk": n,
     }
     starts, total = {}, 0
     for kind, size in sizes.items():
         starts[kind] = total
         total += size
-    return starts, total
+    return list(sizes), starts, total
 
 
 def pair_kernel(
     n, width,
     hid, une, w1, w2, gains, survive, lengths, assign, advantage, base, gap,
-    dw1_out, dw2_out,
-    dw1, dw2, xs, us, xg, wv1, wv2, b0f, a1f, b0g, gx, mp, mr, mk, part, own, rin, p0, dp1, gz, ga, gb, gc,
+    dw1, dw2,
+    xs, us, xg, wv1, wv2, b0f, a1f, b0g, gx, mp, mr, mk, part, own, rin, p0, dp1, gz, ga, gb, gc,
     wr, wsend, ps, psr, scs, scr, inn, inr, sc, rinfo, tok, tk,
     ss, rs, ls,
 ):
@@ -534,7 +534,8 @@
     right = {"dp": j + 1}
     left = {"dp": j - 1}
     lane = lax.broadcasted_iota(jnp.int32, (rows, LANES), 1)
-    starts, _ = pair_slots(n)
+    kinds, starts, _ = pair_slots(n)
+    most = pl.ds(0, (n - 1) * rows)
 
     def blk(b):
         return pl.ds(pl.multiple_of(b * rows, rows), rows)
@@ -548,25 +549,24 @@
     def mrows(g, b):
         return pl.ds(pl.multiple_of(g * v + b * mb, mb), mb)
 
-    def send(kind, si, ri, a, b, dev):
-        k = starts[kind]
+    def send(kind, ri, a, b, dev):
+        slot = kinds.index("rr" if kind == "rl" else kind)
         pltpu.make_async_remote_copy(
-            src_ref=a, dst_ref=b, send_sem=ss.at[k + si], recv_sem=rs.at[k + ri],
+            src_ref=a, dst_ref=b, send_sem=ss.at[slot], recv_sem=rs.at[starts[kind] + ri],
             device_id=dev, device_id_type=pl.DeviceIdType.MESH,
         ).start()
 
-    def handle(kind, i, a):
-        k = starts[kind]
-        return pltpu.make_async_remote_copy(
-            src_ref=a, dst_ref=a, send_sem=ss.at[k + i], recv_sem=rs.at[k + i],
+    def got(kind, i, a):
+        pltpu.make_async_remote_copy(
+            src_ref=a, dst_ref=a, send_sem=ss.at[kinds.index(kind)], recv_sem=rs.at[starts[kind] + i],
             device_id=partner, device_id_type=pl.DeviceIdType.MESH,
-        )
-
-    def got(kind, i, a):
-        handle(kind, i, a).wait_recv()
-
-    def sent(kind, i, a):
-        handle(kind, i, a).wait_send()
+        ).wait_recv()
+
+    def sent(kind, a):
+        pltpu.make_async_remote_copy(
+            src_ref=a, dst_ref=a, send_sem=ss.at[kinds.index(kind)], recv_sem=rs.at[0],
+            device_id=partner, device_id_type=pl.DeviceIdType.MESH,
+        ).wait_send()
 
     def others(body):
         def step(k, carry):
@@ -596,7 +596,7 @@
             kept = jnp.where(inside, survive[0:1, g:g + 1].astype(F32), kept)
         held = jnp.sum(kept * lengths[...].astype(F32), axis=1, keepdims=True)
         tok[...] = jnp.broadcast_to(held, (8, LANES))
-        others(lambda b: send("tk", b, j, tok, tk.at[j], {"dp": b}))
+        others(lambda b: send("tk", j, tok, tk.at[j], {"dp": b}))
         tk[j] = tok[...]
 
     def tokens():
@@ -640,7 +640,7 @@
             if not at_end:
                 got(kind, slot + r, rin.at[way, q, r])
                 part[q, r] = (part[q, r].astype(F32) + rin[way, q, r].astype(F32)).astype(BF)
-            send(kind, slot + r, slot + r, part.at[q, r], rin.at[way, q, r], dev)
+            send(kind, slot + r, part.at[q, r], rin.at[way, q, r], dev)
 
         first = j == 0 if at_end else (j > 0) & (j + d < n)
         final = j == n - 1 if at_end else (j < n - 1) & (j - d >= 0)
@@ -664,14 +664,9 @@
             got("rl", slot, rin.at[1, q, j])
             own[q] += rin[1, q, j].astype(F32)
 
-    def reduce_sent(q):
-        for d in range(1, n):
-            pl.when(j + d < n)(lambda: sent("rr", q * n + j + d, part.at[q, j + d]))
-            pl.when(j - d >= 0)(lambda: sent("rl", q * n + j - d, part.at[q, j - d]))
-
     def gather(kind, at):
         for d in range(n - 1, 0, -1):
-            at_distance(d, lambda b: send(kind, b, j, at(j), at(j), {"dp": b}))
+            at_distance(d, lambda b: send(kind, j, at(j), at(j), {"dp": b}))
 
     def at_p0(b):
         return p0.at[t, blk(b)]
@@ -691,7 +686,7 @@
         return unpack(sums)[:, 0:1]
 
     def gram_send():
-        others(lambda b: send("mr", b, j, mp.at[b], mr.at[j], {"dp": b}))
+        others(lambda b: send("mr", j, mp.at[b], mr.at[j], {"dp": b}))
 
     def gram_reduce():
         mr[j] = mp[j]
@@ -701,14 +696,14 @@
             total = total + mr[b].astype(F32)
         mk[mrows(y, j)] = total.astype(BF)
         here = mk.at[mrows(y, j)]
-        others(lambda b: send("mk", b, j, here, here, {"dp": b}))
-        send("my", j, j, here, here, {"groups": 1 - y})
+        others(lambda b: send("mk", j, here, here, {"dp": b}))
+        send("my", j, here, here, {"groups": 1 - y})
 
     def gram_pass():
         def across(b):
             here = mk.at[mrows(y, b)]
             got("mk", b, here)
-            send("my", b, b, here, here, {"groups": 1 - y})
+            send("my", b, here, here, {"groups": 1 - y})
         others(across)
 
     def gram_wait():
@@ -722,7 +717,7 @@
 
     def main_send(src, main, d):
         at_distance(d, lambda b: send(
-            "a", b, j, src.at[:, wide(b, t)], main.at[blk(j), cols(t)], {"dp": b}
+            "a", j, src.at[:, wide(b, t)], main.at[blk(j), cols(t)], {"dp": b}
         ))
 
     def main_start(src, other_src, main, other):
@@ -739,17 +734,20 @@
         def first(b):
             here = main.at[blk(b), cols(t)]
             got("a", b, here)
-            send("ax", b, b, here, here, {"section": 1 - s})
-            send("af", b, b, here, here, partner)
+            send("ax", b, here, here, {"section": 1 - s})
+            send("af", b, here, here, partner)
         at_distance(d, first)
         at_distance(d, lambda b: got("af", b, main.at[blk(b), cols(o)]))
 
-    def other_arrive(other, d):
+    def other_take(other):
         def first(b):
             here = other.at[blk(b), cols(t)]
             got("ax", b, here)
-            send("axf", b, b, here, here, partner)
-        at_distance(d, first)
+            send("axf", b, here, here, partner)
+        for d in range(n - 1, 0, -1):
+            at_distance(d, first)
+
+    def other_arrive(other, d):
         at_distance(d, lambda b: got("axf", b, other.at[blk(b), cols(o)]))
 
     barrier = pltpu.get_barrier_semaphore()
@@ -765,23 +763,19 @@
         greet({"section": 1 - s, "tensor": o})
         pl.semaphore_wait(barrier, n + 3)
 
-    def drain_common(main, other):
-        def one(b):
-            sent("a", b, main.at[blk(b), cols(t)])
-            sent("ax", b, main.at[blk(b), cols(t)])
-            sent("af", b, main.at[blk(b), cols(t)])
-            sent("axf", b, other.at[blk(b), cols(t)])
-            sent("mr", b, mp.at[b])
-            sent("ps", b, ps.at[b])
-            sent("tk", b, tk.at[b])
-            sent("g0f", b, at_p0(b))
-            sent("g2", b, at_gz(b))
-            sent("gs", b, sc.at[b])
-        others(one)
-        others(lambda b: sent("mk", b, mk.at[mrows(y, j)]))
-        for b in range(n):
-            sent("my", b, mk.at[mrows(y, b)])
-        sent("bf", 0, b0f.at[t])
+    def drain_common(main, other, sums):
+        for kind in ("a", "ax", "af"):
+            sent(kind, main.at[most, pl.ds(0, half)])
+        sent("axf", other.at[most, pl.ds(0, half)])
+        sent("mr", mp.at[pl.ds(0, n - 1)])
+        sent("mk", mk.at[pl.ds(0, (n - 1) * mb)])
+        sent("my", mk.at[pl.ds(0, n * mb)])
+        sent("ps", ps.at[pl.ds(0, n - 1)])
+        sent("tk", tk.at[pl.ds(0, n - 1)])
+        sent("gs", sc.at[pl.ds(0, n - 1)])
+        sent("rr", part.at[pl.ds(0, sums), pl.ds(0, n - 1)])
+        sent("g0f", gz.at[most])
+        sent("bf", b0f.at[t])
 
     def first_section():
         local_copy(2, w1, wv1).start()
@@ -789,10 +783,11 @@
         meet()
         @pl.when(t == y)
         def _():
-            send("bx", 0, 0, w2, b0f.at[t], {"section": 1})
+            send("bx", 0, w2, b0f.at[t], {"section": 1})
         main_start(hid, une, xs, us)
-        send("bf", 0, 0, w2, b0f.at[t], partner)
+        send("bf", 0, w2, b0f.at[t], partner)
         own_tokens()
+        row_info()
         local_copy(2, w1, wv1).wait()
         local_copy(3, w2, b0f.at[t]).wait()
         main_wait(hid, une, xs, us)
@@ -807,7 +802,7 @@
             pa, pb = project(b)
             part[0, b] = pa.astype(BF)
             part[1, b] = pb.astype(BF)
-            send("ps", b, j, ps.at[b], psr.at[j], {"dp": b})
+            send("ps", j, ps.at[b], psr.at[j], {"dp": b})
 
         def project_other(b):
             part[2, b] = dot(us[blk(b)], b0f[t], 1, 1).astype(BF)
@@ -826,6 +821,7 @@
         reduce_inner(0, n - 2)
         reduce_inner(1, n - 2, 2)
         gram_reduce()
+        other_take(us)
         for d in range(n - 1, 0, -1):
             other_arrive(us, d)
             at_distance(d, project_other)
@@ -835,18 +831,19 @@
         xx = scalar_sums()
         inverse = lax.rsqrt(xx / width + eps_norm)
         p0[t, blk(j)] = (inverse * own[0]).astype(BF)
-        send("p0", 0, t, at_p0(j), at_p0(j), partner)
+        send("p0", t, at_p0(j), at_p0(j), partner)
         for c in range(2):
-            send("p0", 1 + c, t, at_p0(j), at_p0(j), {"section": 1, "tensor": c})
+            send("p0", t, at_p0(j), at_p0(j), {"section": 1, "tensor": c})
         reduce_inner(2, n - 2, 2)
         gram_pass()
         reduce_inner(2, 1)
+        gather("g0", at_p0)
 
         @pl.when(t == y)
         def _():
             got("ax1", 0, a1f.at[t])
-            send("ay", 0, 0, a1f.at[t], a1f.at[t], {"groups": 1 - y})
-            send("af1", 0, 0, a1f.at[t], a1f.at[t], partner)
+            send("ay", 0, a1f.at[t], a1f.at[t], {"groups": 1 - y})
+            send("af1", 0, a1f.at[t], a1f.at[t], partner)
         reduce_own(1)
         reduce_own(2)
         gram_wait()
@@ -854,41 +851,51 @@
         kb = own[1] + dot(p0[0, blk(j)], mk[0:v]) + dot(p0[1, blk(j)], mk[v:2 * v])
         p0v = p0[t, blk(j)].astype(F32)
         scs[...] = pack([
-            xx,
             jnp.sum(p0v * (own[1] + kb), axis=1, keepdims=True),
             jnp.sum(p0v * own[2], axis=1, keepdims=True),
         ])
-        for c in range(2):
-            send("s0", c, t, scs, scr.at[t], {"section": 1, "tensor": c})
-        gather("g0", at_p0)
+        send("s0", 0, scs, scr, partner)
         own[1] = kb
         got("w", 0, wr.at[0])
         got("w", 1, wr.at[1])
-        got("s1", 0, sc.at[j])
-        others(lambda b: send("gs", b, j, sc.at[j], sc.at[j], {"dp": b}))
-        packed = unpack(sc[j])
-        grad = packed[:, 0:1] * own[2] - packed[:, 2:3] * own[1]
-        grad += packed[:, 1:2] * (wr[0].astype(F32) + wr[1].astype(F32))
+        got("in", 0, inr.at[0])
+        got("in", 1, inr.at[1])
+        got("s0", 0, scr)
+        sums = unpack(scs[...] + scr[...])
+        squares = xx + sums[:, 0:1]
+        raised_inverse = lax.rsqrt(jnp.maximum(squares, 0.0) / width + eps_norm)
+        inner = unpack(inr[0] + inr[1])[:, 0:2]
+        logit = 0.5 * inner[:, 1:2] + sums[:, 1:2] + raised_inverse * inner[:, 0:1]
+        weight = rinfo[:, 0:1]
+        seed = jnp.where(weight == 0.0, 0.0, weight * jnp.exp(logit - rinfo[:, 1:2]))
+        scaled = seed * raised_inverse
+        pull = raised_inverse * raised_inverse * raised_inverse * (seed * inner[:, 0:1]) / width
+        grad = seed * own[2] - pull * own[1] + scaled * (wr[0].astype(F32) + wr[1].astype(F32))
         gz[blk(j)] = (inverse * grad).astype(BF)
+        sc[j] = pack([seed, scaled, pull])
+        send("s1", 0, sc.at[j], sc.at[j], {"section": 1})
+        others(lambda b: send("gs", j, sc.at[j], sc.at[j], {"dp": b}))
         gather("g2", at_gz)
 
         def pass_p0(b):
             got("g0", b, at_p0(b))
-            send("g0f", b, b, at_p0(b), at_p0(b), partner)
-            send("g0x", b, b, at_p0(b), at_p0(b), {"section": 1})
-        others(pass_p0)
+            send("g0f", b, at_p0(b), at_p0(b), partner)
+            send("g0x", b, at_p0(b), at_p0(b), {"section": 1})
+        for d in range(1, n):
+            at_distance(d, pass_p0)
 
         @pl.when(t != y)
         def _():
             got("ay", 0, a1f.at[t])
-            send("af1", 0, 0, a1f.at[t], a1f.at[t], partner)
+            send("af1", 0, a1f.at[t], a1f.at[t], partner)
         got("gn", 0, gx)
         scale = tokens()
 
         def pass_dp1(b):
             got("gx", b, at_dp1(b))
-            send("g1f", b, b, at_dp1(b), at_dp1(b), partner)
-        others(pass_dp1)
+            send("g1f", b, at_dp1(b), at_dp1(b), partner)
+        for d in range(1, n):
+            at_distance(d, pass_dp1)
         others(lambda b: got("g0f", b, p0.at[o, blk(b)]))
         got("d1", t, at_dp1(j))
         got("d1", o, dp1.at[o, blk(j)])
@@ -909,28 +916,22 @@
         for h in range(2):
             dw2[...] += dot(dot(p0[t], gb[h], 0, 0).astype(BF), b0f[h])
         dw2[...] = (dw2[...] + dot(ga[...], us[...], 0, 0) + dot(gb[t], xs[...], 0, 0)) * scale
-        local_copy(1, dw2, dw2_out).start()
         others(lambda b: got("g2", b, at_gz(b)))
         dw1[...] = dot(xg[...], gz[...], 0, 0) * scale
-        local_copy(0, dw1, dw1_out).start()
-        drain_common(xs, us)
+        drain_common(xs, us, 3)
 
         @pl.when(t == y)
         def _():
-            sent("bx", 0, b0f.at[t])
-            sent("ay", 0, a1f.at[t])
-        sent("af1", 0, a1f.at[t])
-        for c in range(3):
-            sent("p0", c, at_p0(j))
-        for c in range(2):
-            sent("s0", c, scs)
-        others(lambda b: sent("g0", b, at_p0(b)))
-        others(lambda b: sent("g0x", b, at_p0(b)))
-        others(lambda b: sent("g1f", b, at_dp1(b)))
-        for q in range(3):
-            reduce_sent(q)
-        local_copy(0, dw1, dw1_out).wait()
-        local_copy(1, dw2, dw2_out).wait()
+            sent("bx", b0f.at[t])
+            sent("ay", a1f.at[t])
+        sent("af1", a1f.at[t])
+        sent("p0", part.at[:, 0])
+        sent("s0", scs)
+        sent("s1", scs)
+        sent("g0", gz.at[most])
+        sent("g2", gz.at[most])
+        sent("g0x", gz.at[most])
+        sent("g1f", gz.at[most])
 
     def second_section():
         local_copy(2, w1, a1f.at[t]).start()
@@ -938,7 +939,6 @@
         meet()
         main_start(une, hid, us, xs)
         own_tokens()
-        row_info()
         local_copy(2, w1, a1f.at[t]).wait()
         local_copy(3, w2, wv2).wait()
         main_wait(une, hid, us, xs)
@@ -954,7 +954,7 @@
 
         def project_other(b):
             part[1, b] = project(b).astype(BF)
-            send("ps", b, j, ps.at[b], psr.at[j], {"dp": b})
+            send("ps", j, ps.at[b], psr.at[j], {"dp": b})
 
         own[0] = dot(us[blk(j)], wv2[...], 1, 1)
         own[1] = project(j)
@@ -964,8 +964,8 @@
             @pl.when(t == y)
             def _():
                 got("bx", 0, b0f.at[t])
-                send("bf", 0, 0, b0f.at[t], b0f.at[t], partner)
-                send("by", 0, 0, b0f.at[t], b0f.at[t], {"groups": 1 - y})
+                send("bf", 0, b0f.at[t], b0f.at[t], partner)
+                send("by", 0, b0f.at[t], b0f.at[t], {"groups": 1 - y})
 
             @pl.when(t != y)
             def _():
@@ -975,7 +975,7 @@
             @pl.when(t != y)
             def _():
                 got("by", 0, b0f.at[t])
-                send("bf", 0, 0, b0f.at[t], b0f.at[t], partner)
+                send("bf", 0, b0f.at[t], b0f.at[t], partner)
 
             @pl.when(t == y)
             def _():
@@ -992,54 +992,47 @@
                 gram_send()
         @pl.when(t == y)
         def _():
-            send("ax1", 0, 0, w1, a1f.at[t], {"section": 0})
-        send("gn", 0, 0, gains.at[j], gx, {"section": 0})
+            send("ax1", 0, w1, a1f.at[t], {"section": 0})
+        send("gn", 0, gains.at[j], gx, {"section": 0})
         reduce_inner(0, n - 2)
         gram_reduce()
+        other_take(xs)
         for d in range(n - 1, 0, -1):
             other_arrive(xs, d)
             at_distance(d, project_other)
             reduce_step(1, d, True)
-        reduce_inner(1, n - 2)
+        reduce_inner(1, n - 2, 2)
+        gram_pass()
+        reduce_inner(1, 1)
         reduce_own(0)
         dp1[t, blk(j)] = own[0].astype(BF)
         for c in range(2):
-            send("d1", c, t, at_dp1(j), at_dp1(j), {"section": 0, "tensor": c})
-        gram_pass()
+            send("d1", t, at_dp1(j), at_dp1(j), {"section": 0, "tensor": c})
         gram_wait()
         back = dot(dp1[t, blk(j)], mk[...], 1, 1).astype(BF)
         for c in range(2):
             wsend[c] = back[:, c * v:(c + 1) * v]
-            send("w", c, t, wsend.at[c], wr.at[t], {"section": 0, "tensor": c})
+            send("w", t, wsend.at[c], wr.at[t], {"section": 0, "tensor": c})
         reduce_own(1)
         dotted = scalar_sums()
         gather("g1", at_dp1)
         got("p0", 0, p0.at[0, blk(j)])
         got("p0", 1, p0.at[1, blk(j)])
         raised = own[1] + dot(p0[0, blk(j)], mk[0:v]) + dot(p0[1, blk(j)], mk[v:2 * v])
-        inn[...] = pack([jnp.sum(raised * own[0], axis=1, keepdims=True)])
-        send("in", 0, 0, inn, inr, partner)
+        inn[...] = pack([jnp.sum(raised * own[0], axis=1, keepdims=True), dotted])
+        for c in range(2):
+            send("in", t, inn, inr.at[t], {"section": 0, "tensor": c})
         gz[blk(j)] = raised.astype(BF)
         gather("g2", at_gz)
-        got("in", 0, inr)
-        got("s0", 0, scr.at[0])
-        got("s0", 1, scr.at[1])
-        inner = unpack(inn[...] + inr[...])[:, 0:1]
-        sums = unpack(scr[0] + scr[1])
-        squares = 0.5 * sums[:, 0:1] + sums[:, 1:2]
-        inverse = lax.rsqrt(jnp.maximum(squares, 0.0) / width + eps_norm)
-        logit = dotted + sums[:, 2:3] + inverse * inner
-        weight = rinfo[:, 0:1]
-        seed = jnp.where(weight == 0.0, 0.0, weight * jnp.exp(logit - rinfo[:, 1:2]))
-        scaled = seed * inverse
-        sc[j] = pack([seed, scaled, inverse * inverse * inverse * (seed * inner) / width])
-        send("s1", 0, 0, sc.at[j], sc.at[j], {"section": 0})
-        others(lambda b: send("gs", b, j, sc.at[j], sc.at[j], {"dp": b}))
 
         def pass_dp1(b):
             got("g1", b, at_dp1(b))
-            send("gx", b, b, at_dp1(b), at_dp1(b), {"section": 0})
-        others(pass_dp1)
+            send("gx", b, at_dp1(b), at_dp1(b), {"section": 0})
+
+        for d in range(1, n):
+            at_distance(d, pass_dp1)
+        got("s1", 0, sc.at[j])
+        others(lambda b: send("gs", j, sc.at[j], sc.at[j], {"dp": b}))
         take_rest()
         for h in range(2):
             b0g[h] = (b0f[h].astype(F32) * gains[j]).astype(BF)
@@ -1047,8 +1040,9 @@
 
         def pass_p0(b):
             got("g0x", b, at_p0(b))
-            send("g0f", b, b, at_p0(b), at_p0(b), partner)
-        others(pass_p0)
+            send("g0f", b, at_p0(b), at_p0(b), partner)
+        for d in range(1, n):
+            at_distance(d, pass_p0)
         others(lambda b: got("g0f", b, p0.at[o, blk(b)]))
         others(lambda b: got("g2", b, at_gz(b)))
         others(lambda b: got("gs", b, sc.at[b]))
@@ -1057,30 +1051,23 @@
             ga[blk(b)] = (scaled * gz[blk(b)].astype(F32)).astype(BF)
             gc[blk(b)] = (scaled * dp1[t, blk(b)].astype(F32)).astype(BF)
         dw2[...] = dot(ga[...], us[...], 0, 0) * scale
-        local_copy(1, dw2, dw2_out).start()
         total = dot(xg[...], gc[...], 0, 0)
         for h in range(2):
             total += dot(b0g[h], dot(p0[h], gc[...], 0, 0).astype(BF), 0, 0)
         dw1[...] = total * scale
-        local_copy(0, dw1, dw1_out).start()
-        drain_common(us, xs)
+        drain_common(us, xs, 2)
 
         @pl.when(t == y)
         def _():
-            sent("ax1", 0, a1f.at[t])
-            sent("by", 0, b0f.at[t])
-        sent("gn", 0, gx)
-        others(lambda b: sent("g1", b, at_dp1(b)))
-        others(lambda b: sent("gx", b, at_dp1(b)))
-        sent("in", 0, inn)
-        sent("s1", 0, sc.at[j])
-        for c in range(2):
-            sent("w", c, wsend.at[c])
-            sent("d1", c, at_dp1(j))
-        for q in range(2):
-            reduce_sent(q)
-        local_copy(0, dw1, dw1_out).wait()
-        local_copy(1, dw2, dw2_out).wait()
+            sent("ax1", a1f.at[t])
+            sent("by", b0f.at[t])
+        sent("gn", gx)
+        sent("g1", gz.at[most])
+        sent("g2", gz.at[most])
+        sent("gx", ga.at[most])
+        sent("in", inr)
+        sent("w", wsend)
+        sent("d1", part.at[pl.ds(0, 2), 0])
 
     pl.when(s == 0)(first_section)
     pl.when(s == 1)(second_section)
@@ -1095,20 +1082,18 @@
     rows = count * positions
     chunk, v = value_proj.shape[1:]
     total = n * rows
-    _, slots = pair_slots(n)
+    kinds, _, slots = pair_slots(n)
     vm = pl.BlockSpec(memory_space=pltpu.VMEM)
     hbm = pl.BlockSpec(memory_space=pl.ANY)
     dw1, dw2 = pl.pallas_call(
         functools.partial(pair_kernel, n, width),
         out_shape=(
-            jax.ShapeDtypeStruct((chunk, v), F32),
-            jax.ShapeDtypeStruct((v, chunk), F32),
+            pltpu.VMEM((chunk, v), F32),
+            pltpu.VMEM((v, chunk), F32),
         ),
         in_specs=[hbm] * 4 + [vm] * 7,
-        out_specs=(hbm, hbm),
+        out_specs=(vm, vm),
         scratch_shapes=[
-            pltpu.VMEM((chunk, v), F32),
-            pltpu.VMEM((v, chunk), F32),
             pltpu.VMEM((total, chunk), BF),
             pltpu.VMEM((total, chunk), BF),
             pltpu.VMEM((total, chunk), BF),
@@ -1135,14 +1120,14 @@
             pltpu.VMEM((n, 8, rows), F32),
             pltpu.VMEM((n, 8, rows), F32),
             pltpu.VMEM((8, rows), F32),
-            pltpu.VMEM((2, 8, rows), F32),
             pltpu.VMEM((8, rows), F32),
             pltpu.VMEM((8, rows), F32),
+            pltpu.VMEM((2, 8, rows), F32),
             pltpu.VMEM((n, 8, rows), F32),
             pltpu.VMEM((rows, LANES), F32),
             pltpu.VMEM((8, LANES), F32),
             pltpu.VMEM((n, 8, LANES), F32),
-            pltpu.SemaphoreType.DMA((slots,)),
+            pltpu.SemaphoreType.DMA((len(kinds),)),
             pltpu.SemaphoreType.DMA((slots,)),
             pltpu.SemaphoreType.DMA((4,)),
         ],

time: 68.9 us -> 62.1 us (0.901)
  the two profiles are of different devices: /device:TPU:9 before, /device:TPU:17 now
where the time goes in v3:
time: 62.1 us; the launch traced here: 61.9 us
  Pallas kernels  58.5 us (94%)
  local copies, waits for them, and re-layouts  2.11 us (3%)
  between operations  1.29 us (2%)
    pallas_call x1, Pallas kernels, local_pair(): pl.pallas_call(functools.partial(pair_kernel, n, width), out_shape=(pltpu...  58.5 us
    unnamed x2, local copies, waits for them, and re-layouts  2.11 us

profile of v3, /device:TPU:17, one launch (start us, length us, event | category | flops | bytes accessed | tf_op | source)
XLA Modules:
  0.0 61.9 jit_solution(15499262475356806197)
XLA Ops:
  1.3 58.5 %shard_map.122 = (f32[1280,256]{1,0:T(8,128)S(1)}, f32[256,1280]{1,0:T(8,128)S(1)}) custom-call(bf16[128,5120]{1,0:T(8,128)(2,1)} %bitcast.16, bf16[128,5120]{1,0:T(8,128)(2,1)} %bitcast.17, bf16[1280,256]{1,0:T(8,128)(2,1)} %bitcast.18, bf16[256,1280]{1,0:T(8,128)(2,1)} %bitcast.19, f32[4,1,1280]{2,1,0:T(1,128)} %bitcast.20, s32[1,1]{1,0:T(1,128)} %bitcast.13.survive, ...), custom_call_target="tpu_custom_call" | custom-call | tf_op jit(solution)/shard_map/pallas_call | solution.py:1088
  59.8 1.1 %copy.15 = f32[1,1280,256]{2,1,0:T(8,128)} copy(f32[1,1280,256]{2,1,0:T(8,128)S(1)} %bitcast.15) | data formatting | bytes 2621440
  60.8 1.1 %copy.16 = f32[1,256,1280]{2,1,0:T(8,128)} copy(f32[1,256,1280]{2,1,0:T(8,128)S(1)} %bitcast.14) | data formatting | bytes 2621440

commit v4 on v3

--- a/solution.py
+++ b/solution.py
@@ -504,6 +504,7 @@
         "a": n, "af": n, "ax": n, "axf": n, "bx": 1, "bf": 1, "by": 1, "ax1": 1, "af1": 1, "ay": 1, "gn": 1,
         "mr": n, "mk": n, "my": n, "rr": 3 * n, "rl": 3 * n, "ps": n, "p0": 2, "s0": 1, "in": 2, "w": 2,
         "d1": 2, "s1": 1, "g0": n, "g0x": n, "g0f": n, "g1": n, "gx": n, "g1f": n, "g2": n, "gs": n, "tk": n,
+        "g0r": 0,
     }
     starts, total = {}, 0
     for kind, size in sizes.items():
@@ -535,6 +536,10 @@
     left = {"dp": j - 1}
     lane = lax.broadcasted_iota(jnp.int32, (rows, LANES), 1)
     kinds, starts, _ = pair_slots(n)
+    near = max(n // 2, 1)
+    relayed = n == 2 * near and 0 < near * (near - 1) <= n
+    side = j // near
+    gate = jnp.where(side == 0, near - 1, near)
     most = pl.ds(0, (n - 1) * rows)
 
     def blk(b):
@@ -549,8 +554,8 @@
     def mrows(g, b):
         return pl.ds(pl.multiple_of(g * v + b * mb, mb), mb)
 
-    def send(kind, ri, a, b, dev):
-        slot = kinds.index("rr" if kind == "rl" else kind)
+    def send(kind, ri, a, b, dev, through=""):
+        slot = kinds.index("rr" if kind == "rl" else kind + through)
         pltpu.make_async_remote_copy(
             src_ref=a, dst_ref=b, send_sem=ss.at[slot], recv_sem=rs.at[starts[kind] + ri],
             device_id=dev, device_id_type=pl.DeviceIdType.MESH,
@@ -667,6 +672,39 @@
     def gather(kind, at):
         for d in range(n - 1, 0, -1):
             at_distance(d, lambda b: send(kind, j, at(j), at(j), {"dp": b}))
+
+    def gather_near(kind, at):
+        if not relayed:
+            return gather(kind, at)
+        across = jnp.where(side == 0, near, near - 1)
+        for d in range(n - 1, 0, -1):
+            at_distance(d, lambda b: pl.when((b // near == side) | (b == across))(
+                lambda: send(kind, j, at(j), at(j), {"dp": b})
+            ))
+
+    def hand_on(kind, at):
+        if not relayed:
+            return
+
+        def one(b):
+            got(kind, b, at(b))
+            for r in range(n):
+                pl.when((r // near == side) & (r != j))(
+                    lambda: send(kind, b, at(b), at(b), {"dp": r}, "r")
+                )
+        for d in range(1, n):
+            at_distance(d, lambda b: pl.when((j == gate) & (b // near != side))(lambda: one(b)))
+
+    def handed(kind, at, b):
+        if not relayed:
+            return got(kind, b, at(b))
+        pl.when((j != gate) | (b // near == side))(lambda: got(kind, b, at(b)))
+
+    def gather_sent(kind, whole):
+        if not relayed:
+            return sent(kind, whole.at[most])
+        sent(kind, whole.at[pl.ds(0, near * rows)])
+        pl.when(j == gate)(lambda: sent(kind + "r", whole.at[pl.ds(0, near * (near - 1) * rows)]))
 
     def at_p0(b):
         return p0.at[t, blk(b)]
@@ -837,13 +875,14 @@
         reduce_inner(2, n - 2, 2)
         gram_pass()
         reduce_inner(2, 1)
-        gather("g0", at_p0)
+        gather_near("g0", at_p0)
 
         @pl.when(t == y)
         def _():
             got("ax1", 0, a1f.at[t])
             send("ay", 0, a1f.at[t], a1f.at[t], {"groups": 1 - y})
             send("af1", 0, a1f.at[t], a1f.at[t], partner)
+        hand_on("g0", at_p0)
         reduce_own(1)
         reduce_own(2)
         gram_wait()
@@ -878,30 +917,14 @@
         gather("g2", at_gz)
 
         def pass_p0(b):
-            got("g0", b, at_p0(b))
+            handed("g0", at_p0, b)
             send("g0f", b, at_p0(b), at_p0(b), partner)
             send("g0x", b, at_p0(b), at_p0(b), {"section": 1})
         for d in range(1, n):
             at_distance(d, pass_p0)
-
-        @pl.when(t != y)
-        def _():
-            got("ay", 0, a1f.at[t])
-            send("af1", 0, a1f.at[t], a1f.at[t], partner)
-        got("gn", 0, gx)
         scale = tokens()
-
-        def pass_dp1(b):
-            got("gx", b, at_dp1(b))
-            send("g1f", b, at_dp1(b), at_dp1(b), partner)
-        for d in range(1, n):
-            at_distance(d, pass_dp1)
+        others(lambda b: got("gs", b, sc.at[b]))
         others(lambda b: got("g0f", b, p0.at[o, blk(b)]))
-        got("d1", t, at_dp1(j))
-        got("d1", o, dp1.at[o, blk(j)])
-        got("af1", 0, a1f.at[o])
-        others(lambda b: got("g1f", b, dp1.at[o, blk(b)]))
-        others(lambda b: got("gs", b, sc.at[b]))
         for b in range(n):
             packed = unpack(sc[b])
             held = p0[t, blk(b)].astype(F32)
@@ -909,13 +932,29 @@
                 gb[h, blk(b)] = (-packed[:, 2:3] * p0[h, blk(b)].astype(F32)).astype(BF)
             ga[blk(b)] = (packed[:, 0:1] * held).astype(BF)
             gc[blk(b)] = (packed[:, 1:2] * held).astype(BF)
+        dw2[...] = dot(ga[...], us[...], 0, 0) + dot(gb[t], xs[...], 0, 0)
+        for h in range(2):
+            dw2[...] += dot(dot(p0[t], gb[h], 0, 0).astype(BF), b0f[h])
+
+        @pl.when(t != y)
+        def _():
+            got("ay", 0, a1f.at[t])
+            send("af1", 0, a1f.at[t], a1f.at[t], partner)
+        got("gn", 0, gx)
+
+        def pass_dp1(b):
+            got("gx", b, at_dp1(b))
+            send("g1f", b, at_dp1(b), at_dp1(b), partner)
+        for d in range(1, n):
+            at_distance(d, pass_dp1)
+        got("d1", t, at_dp1(j))
+        got("d1", o, dp1.at[o, blk(j)])
+        got("af1", 0, a1f.at[o])
+        others(lambda b: got("g1f", b, dp1.at[o, blk(b)]))
         through = jnp.zeros((v, chunk), F32)
         for h in range(2):
             through += dot(dot(gc[...], dp1[h], 0, 0).astype(BF), a1f[h], 1, 1)
-        dw2[...] = gx[...] * through
-        for h in range(2):
-            dw2[...] += dot(dot(p0[t], gb[h], 0, 0).astype(BF), b0f[h])
-        dw2[...] = (dw2[...] + dot(ga[...], us[...], 0, 0) + dot(gb[t], xs[...], 0, 0)) * scale
+        dw2[...] = (dw2[...] + gx[...] * through) * scale
         others(lambda b: got("g2", b, at_gz(b)))
         dw1[...] = dot(xg[...], gz[...], 0, 0) * scale
         drain_common(xs, us, 3)
@@ -928,7 +967,7 @@
         sent("p0", part.at[:, 0])
         sent("s0", scs)
         sent("s1", scs)
-        sent("g0", gz.at[most])
+        gather_sent("g0", gz)
         sent("g2", gz.at[most])
         sent("g0x", gz.at[most])
         sent("g1f", gz.at[most])
@@ -1006,8 +1045,6 @@
         reduce_inner(1, 1)
         reduce_own(0)
         dp1[t, blk(j)] = own[0].astype(BF)
-        for c in range(2):
-            send("d1", t, at_dp1(j), at_dp1(j), {"section": 0, "tensor": c})
         gram_wait()
         back = dot(dp1[t, blk(j)], mk[...], 1, 1).astype(BF)
         for c in range(2):
@@ -1022,6 +1059,8 @@
         inn[...] = pack([jnp.sum(raised * own[0], axis=1, keepdims=True), dotted])
         for c in range(2):
             send("in", t, inn, inr.at[t], {"section": 0, "tensor": c})
+        for c in range(2):
+            send("d1", t, at_dp1(j), at_dp1(j), {"section": 0, "tensor": c})
         gz[blk(j)] = raised.astype(BF)
         gather("g2", at_gz)
 

time: 62.1 us -> 60.3 us (0.971)
  the two profiles are of different devices: /device:TPU:17 before, /device:TPU:0 now
where the time goes in v4:
time: 60.3 us; the launch traced here: 59.4 us
  Pallas kernels  56 us (93%)
  local copies, waits for them, and re-layouts  2.11 us (3%)
  between operations  1.29 us (2%)
    pallas_call x1, Pallas kernels, local_pair(): pl.pallas_call(functools.partial(pair_kernel, n, width), out_shape=(pltpu...  56 us
    unnamed x2, local copies, waits for them, and re-layouts  2.11 us

profile of v4, /device:TPU:0, one launch (start us, length us, event | category | flops | bytes accessed | tf_op | source)
XLA Modules:
  0.0 59.4 jit_solution(289266658289842325)
XLA Ops:
  1.3 56.0 %shard_map.122 = (f32[1280,256]{1,0:T(8,128)S(1)}, f32[256,1280]{1,0:T(8,128)S(1)}) custom-call(bf16[128,5120]{1,0:T(8,128)(2,1)} %bitcast.16, bf16[128,5120]{1,0:T(8,128)(2,1)} %bitcast.17, bf16[1280,256]{1,0:T(8,128)(2,1)} %bitcast.18, bf16[256,1280]{1,0:T(8,128)(2,1)} %bitcast.19, f32[4,1,1280]{2,1,0:T(1,128)} %bitcast.20, s32[1,1]{1,0:T(1,128)} %bitcast.13.survive, ...), custom_call_target="tpu_custom_call" | custom-call | tf_op jit(solution)/shard_map/pallas_call | solution.py:1127
  57.3 1.1 %copy.15 = f32[1,1280,256]{2,1,0:T(8,128)} copy(f32[1,1280,256]{2,1,0:T(8,128)S(1)} %bitcast.15) | data formatting | bytes 2621440
  58.3 1.1 %copy.16 = f32[1,256,1280]{2,1,0:T(8,128)} copy(f32[1,256,1280]{2,1,0:T(8,128)S(1)} %bitcast.14) | data formatting | bytes 2621440

commit v5 on v4

--- a/solution.py
+++ b/solution.py
@@ -502,8 +502,8 @@
 def pair_slots(n):
     sizes = {
         "a": n, "af": n, "ax": n, "axf": n, "bx": 1, "bf": 1, "by": 1, "ax1": 1, "af1": 1, "ay": 1, "gn": 1,
-        "mr": n, "mk": n, "my": n, "rr": 3 * n, "rl": 3 * n, "ps": n, "p0": 2, "s0": 1, "in": 2, "w": 2,
-        "d1": 2, "s1": 1, "g0": n, "g0x": n, "g0f": n, "g1": n, "gx": n, "g1f": n, "g2": n, "gs": n, "tk": n,
+        "mr": 1, "mk": n, "my": 1, "rr": 3 * n, "rl": 3 * n, "ps": 1, "p0": 2, "s0": 1, "in": 2, "w": 2,
+        "d1": 2, "s1": 1, "g0": n, "g0x": n, "g0f": 1, "g1": n, "gx": n, "g1f": 1, "g2": 1, "gs": 1, "tk": 1,
         "g0r": 0,
     }
     starts, total = {}, 0
@@ -556,6 +556,8 @@
 
     def send(kind, ri, a, b, dev, through=""):
         slot = kinds.index("rr" if kind == "rl" else kind + through)
+        if kind in ("mr", "my", "ps", "g0f", "g1f", "g2", "gs", "tk"):
+            ri = 0
         pltpu.make_async_remote_copy(
             src_ref=a, dst_ref=b, send_sem=ss.at[slot], recv_sem=rs.at[starts[kind] + ri],
             device_id=dev, device_id_type=pl.DeviceIdType.MESH,
@@ -605,7 +607,7 @@
         tk[j] = tok[...]
 
     def tokens():
-        others(lambda b: got("tk", b, tk.at[b]))
+        got("tk", 0, tk.at[pl.ds(0, n - 1)])
         total = tk[0]
         for b in range(1, n):
             total = total + tk[b]
@@ -717,7 +719,7 @@
 
     def scalar_sums():
         psr[j] = ps[j]
-        others(lambda b: got("ps", b, psr.at[b]))
+        got("ps", 0, psr.at[pl.ds(0, n - 1)])
         sums = psr[0]
         for b in range(1, n):
             sums = sums + psr[b]
@@ -728,7 +730,7 @@
 
     def gram_reduce():
         mr[j] = mp[j]
-        others(lambda b: got("mr", b, mr.at[b]))
+        got("mr", 0, mr.at[pl.ds(0, n - 1)])
         total = mr[0].astype(F32)
         for b in range(1, n):
             total = total + mr[b].astype(F32)
@@ -745,8 +747,7 @@
         others(across)
 
     def gram_wait():
-        for b in range(n):
-            got("my", b, mk.at[mrows(1 - y, b)])
+        got("my", 0, mk.at[pl.ds(0, n * mb)])
 
     def store_gram(value):
         value = value.astype(BF)
@@ -923,8 +924,8 @@
         for d in range(1, n):
             at_distance(d, pass_p0)
         scale = tokens()
-        others(lambda b: got("gs", b, sc.at[b]))
-        others(lambda b: got("g0f", b, p0.at[o, blk(b)]))
+        got("gs", 0, sc.at[pl.ds(0, n - 1)])
+        got("g0f", 0, p0.at[o, most])
         for b in range(n):
             packed = unpack(sc[b])
             held = p0[t, blk(b)].astype(F32)
@@ -950,12 +951,12 @@
         got("d1", t, at_dp1(j))
         got("d1", o, dp1.at[o, blk(j)])
         got("af1", 0, a1f.at[o])
-        others(lambda b: got("g1f", b, dp1.at[o, blk(b)]))
+        got("g1f", 0, dp1.at[o, most])
         through = jnp.zeros((v, chunk), F32)
         for h in range(2):
             through += dot(dot(gc[...], dp1[h], 0, 0).astype(BF), a1f[h], 1, 1)
         dw2[...] = (dw2[...] + gx[...] * through) * scale
-        others(lambda b: got("g2", b, at_gz(b)))
+        got("g2", 0, gz.at[most])
         dw1[...] = dot(xg[...], gz[...], 0, 0) * scale
         drain_common(xs, us, 3)
 
@@ -1082,9 +1083,9 @@
             send("g0f", b, at_p0(b), at_p0(b), partner)
         for d in range(1, n):
             at_distance(d, pass_p0)
-        others(lambda b: got("g0f", b, p0.at[o, blk(b)]))
-        others(lambda b: got("g2", b, at_gz(b)))
-        others(lambda b: got("gs", b, sc.at[b]))
+        got("g0f", 0, p0.at[o, most])
+        got("g2", 0, gz.at[most])
+        got("gs", 0, sc.at[pl.ds(0, n - 1)])
         for b in range(n):
             scaled = unpack(sc[b])[:, 1:2]
             ga[blk(b)] = (scaled * gz[blk(b)].astype(F32)).astype(BF)

time: 60.3 us -> 60.1 us (level)
  no operation moved by 1% of the time
where the time goes in v5:
time: 60.1 us; the launch traced here: 59.2 us
  Pallas kernels  55.8 us (93%)
  local copies, waits for them, and re-layouts  2.11 us (4%)
  between operations  1.29 us (2%)
    pallas_call x1, Pallas kernels, local_pair(): pl.pallas_call(functools.partial(pair_kernel, n, width), out_shape=(pltpu...  55.8 us
    unnamed x2, local copies, waits for them, and re-layouts  2.11 us

profile of v5, /device:TPU:0, one launch (start us, length us, event | category | flops | bytes accessed | tf_op | source)
XLA Modules:
  0.0 59.2 jit_solution(6161178634615652547)
XLA Ops:
  1.3 55.8 %shard_map.122 = (f32[1280,256]{1,0:T(8,128)S(1)}, f32[256,1280]{1,0:T(8,128)S(1)}) custom-call(bf16[128,5120]{1,0:T(8,128)(2,1)} %bitcast.16, bf16[128,5120]{1,0:T(8,128)(2,1)} %bitcast.17, bf16[1280,256]{1,0:T(8,128)(2,1)} %bitcast.18, bf16[256,1280]{1,0:T(8,128)(2,1)} %bitcast.19, f32[4,1,1280]{2,1,0:T(1,128)} %bitcast.20, s32[1,1]{1,0:T(1,128)} %bitcast.13.survive, ...), custom_call_target="tpu_custom_call" | custom-call | tf_op jit(solution)/shard_map/pallas_call | solution.py:1128
  57.1 1.1 %copy.15 = f32[1,1280,256]{2,1,0:T(8,128)} copy(f32[1,1280,256]{2,1,0:T(8,128)S(1)} %bitcast.15) | data formatting | bytes 2621440
  58.1 1.1 %copy.16 = f32[1,256,1280]{2,1,0:T(8,128)} copy(f32[1,256,1280]{2,1,0:T(8,128)S(1)} %bitcast.14) | data formatting | bytes 2621440
